TPU v7x, 32 devices: a 4x4x1 block of a 4x4x8 slice. The times are simulated.
32 devices in a mesh: dp: 1 (over z), cp: 4 (over y), tp: 8 (over x, core).
Axes of the slice: x: 4, y: 4, z: 1, core: 2. Of those that a mesh axis runs over, the one named last changes fastest.
The devices are a block of a 4x4x8 slice.
Arguments:
- hidden_in: bfloat16 [6144, 2048], P(('dp', 'cp', 'tp'))
- w_query: bfloat16 [2048, 16, 128], P(None, 'tp')
- w_key: bfloat16 [2048, 16, 128], P(None, 'tp')
- w_value: bfloat16 [2048, 16, 128], P(None, 'tp')
- w_out: bfloat16 [16, 128, 2048], P('tp')
- expert_idx: int32 [6144, 8], P(('dp', 'cp', 'tp'))
- gate_vals: float32 [6144, 8], P(('dp', 'cp', 'tp'))
- w_gate: bfloat16 [64, 2048, 1024], P(('cp', 'tp'))
- w_up: bfloat16 [64, 2048, 1024], P(('cp', 'tp'))
- w_down: bfloat16 [64, 1024, 2048], P(('cp', 'tp'))
Outputs:
- output: bfloat16 [6144, 2048], P(('dp', 'cp', 'tp'))
All inputs are finite; a program needn't handle non-finite values.
Results may differ from a plain program's by a relative error of at most 0.0150772.
Values are sent between devices in bfloat16 or wider.
A program may use at most 768 MiB of HBM per device.

v0:
```python
import math
import jax
import jax.numpy as jnp
from jax import lax
from jax.sharding import PartitionSpec as P


def row_positions(row_ids, block_rows, cp_devs):
    chunk_rows = block_rows // 2
    block_id = row_ids // block_rows
    offset_in = row_ids % block_rows
    return jnp.where(offset_in < chunk_rows, block_id * chunk_rows + offset_in, (2 * cp_devs - 1 - block_id) * chunk_rows + offset_in - chunk_rows)


def attend_blocks(query_vecs, key_all, value_all, q_position, k_position):
    row_count, kv_heads, group_size, head_dim = query_vecs.shape
    q_block = math.gcd(row_count, 128)
    n_blocks = row_count // q_block
    score_scale = head_dim ** -0.5

    def one_block(operands):
        q_blk, q_place = operands
        scores = jnp.einsum('qgrd,kgd->qgrk', q_blk, key_all, preferred_element_type=jnp.float32) * score_scale
        allowed = k_position[None, None, None, :] <= q_place[:, None, None, None]
        scores = jnp.where(allowed, scores, -1e30)
        attn_prob = jax.nn.softmax(scores, axis=-1).astype(jnp.bfloat16)
        attn_out = jnp.einsum('qgrk,kgd->qgrd', attn_prob, value_all, preferred_element_type=jnp.float32)
        return attn_out.astype(jnp.bfloat16)

    blocks = lax.map(one_block, (query_vecs.reshape(n_blocks, q_block, kv_heads, group_size, head_dim), q_position.reshape(n_blocks, q_block)))
    return blocks.reshape(row_count, kv_heads * group_size * head_dim)


def attention_residual(hidden_in, w_query, w_key, w_value, w_out, cp_devs):
    hidden = hidden_in.shape[1]
    kv_heads = w_key.shape[1]
    head_dim = w_key.shape[2]
    group_size = w_query.shape[1] // kv_heads
    gathered = lax.all_gather(hidden_in, 'tp', axis=0, tiled=True)
    block_rows = gathered.shape[0]
    query_vecs = jnp.dot(gathered, w_query.reshape(hidden, -1), preferred_element_type=jnp.float32).astype(jnp.bfloat16).reshape(block_rows, kv_heads, group_size, head_dim)
    key_loc = jnp.dot(gathered, w_key.reshape(hidden, -1), preferred_element_type=jnp.float32).astype(jnp.bfloat16)
    value_loc = jnp.dot(gathered, w_value.reshape(hidden, -1), preferred_element_type=jnp.float32).astype(jnp.bfloat16)
    key_all = lax.all_gather(key_loc, 'cp', axis=0, tiled=True).reshape(-1, kv_heads, head_dim)
    value_all = lax.all_gather(value_loc, 'cp', axis=0, tiled=True).reshape(-1, kv_heads, head_dim)
    cp_rank = lax.axis_index('cp')
    q_position = row_positions(cp_rank * block_rows + jnp.arange(block_rows), block_rows, cp_devs)
    k_position = row_positions(jnp.arange(block_rows * cp_devs), block_rows, cp_devs)
    attn_all = attend_blocks(query_vecs, key_all, value_all, q_position, k_position)
    part_sum = jnp.dot(attn_all, w_out.reshape(-1, hidden), preferred_element_type=jnp.float32)
    reduced = lax.psum_scatter(part_sum, 'tp', scatter_dimension=0, tiled=True)
    return (hidden_in.astype(jnp.float32) + reduced).astype(jnp.bfloat16)


def solution(mesh):
    cp_devs = mesh.shape['cp']
    group_devs = cp_devs * mesh.shape['tp']
    row_spec = P(('dp', 'cp', 'tp'), None)
    head_spec = P(None, 'tp', None)
    expert_spec = P(('cp', 'tp'), None, None)

    def device_step(hidden_in, w_query, w_key, w_value, w_out, expert_idx, gate_vals, w_gate, w_up, w_down):
        tok_dev, hidden = hidden_in.shape
        top_k = expert_idx.shape[1]
        local_exp = w_gate.shape[0]
        experts = local_exp * group_devs
        capacity = tok_dev * top_k // experts
        resid_h = attention_residual(hidden_in, w_query, w_key, w_value, w_out, cp_devs)
        flat_idx = expert_idx.reshape(-1)
        hit_mask = flat_idx[:, None] == jnp.arange(experts)[None, :]
        slot_all = jnp.cumsum(hit_mask.astype(jnp.int32), axis=0) - 1
        slot_ids = jnp.sum(jnp.where(hit_mask, slot_all, 0), axis=1)
        dest_row = flat_idx * capacity + slot_ids
        src_rows = jnp.zeros((experts * capacity,), jnp.int32).at[dest_row].set(jnp.arange(tok_dev * top_k, dtype=jnp.int32) // top_k)
        send_buf = jnp.take(resid_h, src_rows, axis=0)
        recv_buf = lax.all_to_all(send_buf, ('cp', 'tp'), 0, 0, tiled=True)
        expert_in = recv_buf.reshape(group_devs, local_exp, capacity, hidden)
        gate_act = jnp.einsum('gech,ehf->gecf', expert_in, w_gate, preferred_element_type=jnp.float32)
        up_act = jnp.einsum('gech,ehf->gecf', expert_in, w_up, preferred_element_type=jnp.float32)
        hidden_act = (jax.nn.silu(gate_act) * up_act).astype(jnp.bfloat16)
        expert_out = jnp.einsum('gecf,efh->gech', hidden_act, w_down, preferred_element_type=jnp.float32).astype(jnp.bfloat16)
        returned = lax.all_to_all(expert_out.reshape(experts * capacity, hidden), ('cp', 'tp'), 0, 0, tiled=True)
        per_choice = jnp.take(returned, dest_row, axis=0).reshape(tok_dev, top_k, hidden)
        moe_sum = jnp.sum(gate_vals[:, :, None] * per_choice, axis=1)
        return (resid_h.astype(jnp.float32) + moe_sum).astype(jnp.bfloat16)

    return jax.shard_map(device_step, mesh=mesh, in_specs=(row_spec, head_spec, head_spec, head_spec, P('tp', None, None), row_spec, row_spec, expert_spec, expert_spec, expert_spec), out_specs=row_spec, check_vma=False)
```

profile of v0, /device:TPU:97, one launch (start us, length us, event | category | flops | bytes accessed | tf_op | source)
XLA Modules:
  0.0 543.1 jit_solution(18319621280782883527)
XLA Ops:
  7.4 43.9 %all-gather.4.cloned.1.call-done = bf16[1536,2048]{1,0:T(8,128)(2,1)} async-done(((bf16[192,2048]{1,0:T(8,128)(2,1)}), bf16[1536,2048]{1,0:T(8,128)(2,1)}) %all-gather.4.cloned.1.call-update) | async-done | bytes 6291472 | tf_op jit(solution)/shard_map/all_gather | solution.py:39
  51.3 5.8 %convolution_convert_fusion = bf16[1536,256]{1,0:T(8,128)(2,1)} fusion(bf16[1536,2048]{1,0:T(8,128)(2,1)} %all-gather.4.cloned.1.call-done, bf16[256,8,2,128]{3,2,1,0:T(2,128)(2,1)} %bitcast.150), kind=kOutput, calls=%fused_computation.57 | convolution fusion | flops 1611005952 | bytes 8126464 | tf_op jit(solution)/shard_map/dot_general | solution.py:43
  57.2 5.5 %convolution_convert_fusion.1 = bf16[1536,256]{1,0:T(8,128)(2,1)} fusion(bf16[1536,2048]{1,0:T(8,128)(2,1)} %all-gather.4.cloned.1.call-done, bf16[256,8,2,128]{3,2,1,0:T(2,128)(2,1)S(1)} %bitcast.151), kind=kOutput, calls=%fused_computation.58 | convolution fusion | flops 1611005952 | bytes 8126464 | tf_op jit(solution)/shard_map/dot_general | solution.py:42
  63.1 4.8 convolution_convert_fusion.2
  68.1 25.4 %all-gather.8.cloned.1.call-done = bf16[6144,256]{1,0:T(8,128)(2,1)} async-done(((bf16[1536,256]{1,0:T(8,128)(2,1)}), bf16[6144,256]{1,0:T(8,128)(2,1)}) %all-gather.8.cloned.1.call-update) | async-done | bytes 3145744 | tf_op jit(solution)/shard_map/all_gather | solution.py:45
  93.6 4.1 copy_bitcast_fusion.2
  97.6 34.5 %all-gather.6.cloned.1.call-done = bf16[6144,256]{1,0:T(8,128)(2,1)} async-done(((bf16[1536,256]{1,0:T(8,128)(2,1)}), bf16[6144,256]{1,0:T(8,128)(2,1)}) %all-gather.6.cloned.1.call-update) | async-done | bytes 3145744 | tf_op jit(solution)/shard_map/all_gather | solution.py:44
  132.1 4.1 copy_bitcast_fusion.3
  136.2 83.9 %while.11 = (s32[]{:T(128)}, bf16[12,128,2,1,128]{4,2,1,0,3:T(2,128)(2,1)S(1)}, s32[12,128]{1,0:T(8,128)S(1)}, bf16[12,128,2,1,128]{4,2,1,0,3:T(2,128)(2,1)S(1)}...) while((s32[]{:T(128)}, ...), condition=%wide.region_3.4_spmd.clone, body=%wide.region_0.3_spmd.clone.sunk | while | flops 818830848 | bytes 39770740 | solution.py:30
  136.8 3.7 fusion.91
  150.8 3.7 fusion.91
  220.2 6.4 %fusion.50 = f32[1536,2048]{1,0:T(8,128)} fusion(bf16[256,2048]{1,0:T(8,128)(2,1)S(1)} %bitcast.139, bf16[192,8,2,128]{3,2,1,0:T(2,128)(2,1)S(1)} %bitcast.145), kind=kOutput, calls=%fused_computation.68 | convolution fusion | flops 1610612736 | bytes 14417920 | tf_op jit(solution)/shard_map/dot_general | solution.py:50
  227.6 18.1 %reduce-window.6 = s32[64,12,128]{2,1,0:T(8,128)S(1)} reduce-window(s32[64,12,128]{2,1,0:T(8,128)S(1)} %fusion.53, s32[]{:T(128)} %constant.106.clone.1), window={size=1x1x128 pad=0_0x0_0x127_0}, to_apply=%region_5.6 | reduce-window | flops 12484608 | bytes 786436 | tf_op jit(solution)/shard_map/reduce-window
  247.0 6.4 %scatter_custom_fusion = s32[1536]{0:T(1024)S(1)} fusion(s32[1536]{0:T(1024)S(1)} %fusion.65, s32[1536]{0:T(1024)S(1)} %add_select_fusion.1, s32[]{:T(128)} %constant.106.clone.1), kind=kCustom, calls=%fused_computation.104 | custom fusion | bytes 6148 | tf_op jit(solution)/shard_map/scatter | solution.py:74
  253.6 43.0 %reduce-scatter.2.cloned.1.call-done = f32[192,2048]{1,0:T(8,128)} async-done(((f32[1536,2048]{1,0:T(8,128)}), f32[192,2048]{1,0:T(8,128)}) %reduce-scatter.2.cloned.1.call-update) | async-done | bytes 1572880 | tf_op jit(solution)/shard_map/reduce_scatter | solution.py:51
  298.2 7.1 %gather_fusion = bf16[1536,2048]{1,0:T(8,128)(2,1)} fusion(bf16[192,2048]{1,0:T(8,128)(2,1)S(1)} %add_convert_fusion.1, s32[2048]{0:T(1024)S(1)} %pad_clamp_fusion.1), kind=kCustom, calls=%fused_computation | custom fusion | bytes 12589056 | tf_op jit(solution)/shard_map/jit(_take)/gather | solution.py:75
  308.7 82.9 %all_to_all.18 = bf16[32,48,2048]{2,1,0:T(8,128)(2,1)S(1)} all-to-all(bf16[32,48,2048]{2,1,0:T(8,128)(2,1)S(1)} %broadcast_select_fusion), channel_id=1, replica_groups=mesh['dp'=1,'cp'=4,'tp'=8] {'cp','tp'}, dimensions={0} | all-to-all | bytes 12582912 | tf_op jit(solution)/shard_map/all_to_all | solution.py:76
  391.6 10.9 %fusion.28 = f32[2,32,24,1024]{3,2,1,0:T(8,128)} fusion(bf16[2,2048,1024]{2,1,0:T(8,128)(2,1)} %param.20, bf16[32,2,24,2048]{3,2,1,0:T(8,128)(2,1)S(1)} %bitcast.142), kind=kOutput, calls=%fused_computation.39 | convolution fusion | flops 6442450944 | bytes 20971520 | tf_op jit(solution)/shard_map/gech,ehf->gecf/dot_general | solution.py:79
  402.5 10.7 %fusion.32 = bf16[32,2,24,1024]{3,2,0,1:T(8,128)(2,1)} fusion(f32[2,32,24,1024]{3,2,1,0:T(8,128)} %fusion.28, bf16[2,2048,1024]{2,1,0:T(8,128)(2,1)S(1)} %bitcast.149, bf16[32,2,24,2048]{3,2,1,0:T(8,128)(2,1)S(1)} %bitcast.143), kind=kOutput, calls=%fused_computation.45 | convolution fusion | flops 6451888128 | bytes 24117248 | tf_op jit(solution)/shard_map/gech,ehf->gecf/dot_general | solution.py:78
  413.2 10.8 %convert_bitcast_fusion = bf16[32,2,24,2048]{3,2,0,1:T(8,128)(2,1)S(1)} fusion(bf16[32,2,24,1024]{3,2,0,1:T(8,128)(2,1)} %fusion.32, bf16[2,1024,2048]{2,1,0:T(8,128)(2,1)} %param.21), kind=kOutput, calls=%fused_computation.51 | convolution fusion | flops 6445596672 | bytes 17825792 | tf_op jit(solution)/shard_map/gecf,efh->gech/dot_general | solution.py:81
  427.2 6.2 %all-to-all-start.1 = ((bf16[32,48,2048]{2,1,0:T(8,128)(2,1)}), bf16[32,48,2048]{2,1,0:T(8,128)(2,1)}, u32[]{:S(2)}, u32[]{:S(2)}) async-start(bf16[32,48,2048]{2,1,0:T(8,128)(2,1)} %bitcast.140), calls=%async_computation.2 | async-start | bytes 12582912 | tf_op jit(solution)/shard_map/all_to_all | solution.py:82
  433.9 77.6 %all-to-all-done.1 = bf16[32,48,2048]{2,1,0:T(8,128)(2,1)} async-done(((bf16[32,48,2048]{2,1,0:T(8,128)(2,1)}), bf16[32,48,2048]{2,1,0:T(8,128)(2,1)}, u32[]{:S(2)}, u32[]{:S(2)}) %all-to-all-start.1) | async-done | bytes 6291488 | tf_op jit(solution)/shard_map/all_to_all | solution.py:82
  511.5 16.4 %gather_fusion.1 = bf16[1536,2048]{1,0:T(8,128)(2,1)} fusion(bf16[1536,2048]{1,0:T(8,128)(2,1)} %bitcast.15, s32[2048]{0:T(1024)S(1)} %pad_clamp_fusion), kind=kCustom, calls=%fused_computation.1 | custom fusion | bytes 12589056 | tf_op jit(solution)/shard_map/jit(_take)/gather | solution.py:83
  527.9 7.6 %multiply_reduce_fusion = f32[192,2048]{1,0:T(8,128)S(1)} fusion(bf16[1536,2048]{1,0:T(8,128)(2,1)} %gather_fusion.1, f32[192,8]{1,0:T(8,128)S(1)} %copy.32, pred[192,8]{1,0:T(8,128)(4,1)S(1)} %copy.38), kind=kLoop, calls=%fused_computation.36 | loop fusion | flops 12189696 | bytes 7872000 | tf_op jit(solution)/shard_map/reduce_sum | solution.py:84
  (175 shorter events, 89.4 us)
Async XLA Ops:
  6.5 213.6 %copy-start = (bf16[2,128,2048]{2,1,0:T(8,128)(2,1)S(1)}, bf16[2,128,2048]{2,1,0:T(8,128)(2,1)}, u32[]{:S(2)}) copy-start(bf16[2,128,2048]{2,1,0:T(8,128)(2,1)} %param.16) | copy-start | bytes 3145732
  6.6 50.7 %copy-start.6 = (bf16[2048,2,128]{2,1,0:T(2,128)(2,1)S(1)}, bf16[2048,2,128]{2,1,0:T(2,128)(2,1)}, u32[]{:S(2)}) copy-start(bf16[2048,2,128]{2,1,0:T(2,128)(2,1)} %param.14) | copy-start | bytes 3145732
  6.6 44.8 %all-gather.4.cloned.1.call-start = ((), (), s32[]{:S(2)}) async-start(), calls=%async_computation.3 | async-start | bytes 7077888 | tf_op jit(solution)/shard_map/all_gather | solution.py:39
  7.3 86.2 %all-gather.8.cloned.1.call-start = ((), (), s32[]{:S(2)}) async-start(), calls=%async_computation.5 | async-start | bytes 3932160 | tf_op jit(solution)/shard_map/all_gather | solution.py:45
  57.2 75.0 %all-gather.6.cloned.1.call-start = ((), (), s32[]{:S(2)}) async-start(), calls=%async_computation.4 | async-start | bytes 3932160 | tf_op jit(solution)/shard_map/all_gather | solution.py:44
  62.8 233.8 %reduce-scatter.2.cloned.1.call-start = ((), (), s32[]{:S(2)}) async-start(), calls=%async_computation.6 | async-start | bytes 14155776 | tf_op jit(solution)/shard_map/reduce_scatter | solution.py:51
  136.8 4.7 copy-start.2
  143.8 4.7 copy-start.2
  150.8 4.7 copy-start.2
  157.8 4.7 copy-start.2
  164.8 4.7 copy-start.2
  171.8 4.7 copy-start.2
  178.8 4.7 copy-start.2
  185.8 4.7 copy-start.2
  192.8 4.7 copy-start.2
  199.8 4.7 copy-start.2
  206.8 4.7 copy-start.2
  213.8 4.7 copy-start.2
  226.6 70.0 %copy-start.3 = (bf16[192,2048]{1,0:T(8,128)(2,1)S(1)}, bf16[192,2048]{1,0:T(8,128)(2,1)}, u32[]{:S(2)}) copy-start(bf16[192,2048]{1,0:T(8,128)(2,1)} %param.12) | copy-start | bytes 2359300
  308.7 93.8 %slice-start = ((s8[8388608]{0:T(1024)(128)(4,1)}), s8[4194304]{0:T(1024)(128)(4,1)S(1)}, s32[]{:S(2)}) async-start(s8[8388608]{0:T(1024)(128)(4,1)} %bitcast.148), calls=%async_computation.7 | async-start | bytes 8388608
  391.6 10.9 %slice-start.1 = ((s8[8388608]{0:T(1024)(128)(4,1)}), s8[4194304]{0:T(1024)(128)(4,1)S(1)}, s32[]{:S(2)}) async-start(s8[8388608]{0:T(1024)(128)(4,1)} %bitcast.148), calls=%async_computation.8 | async-start | bytes 8388608
  427.2 6.6 %copy-start.5 = (f32[192,8]{0,1:T(8,128)S(1)}, f32[192,8]{0,1:T(8,128)}, u32[]{:S(2)}) copy-start(f32[192,8]{0,1:T(8,128)} %param.18) | copy-start | bytes 18436
  427.2 84.3 %all-to-all-start.1 = ((bf16[32,48,2048]{2,1,0:T(8,128)(2,1)}), bf16[32,48,2048]{2,1,0:T(8,128)(2,1)}, u32[]{:S(2)}, u32[]{:S(2)}) async-start(bf16[32,48,2048]{2,1,0:T(8,128)(2,1)} %bitcast.140), calls=%async_computation.2 | async-start | bytes 12582912 | tf_op jit(solution)/shard_map/all_to_all | solution.py:82
  511.5 25.1 %copy-start.1 = (bf16[2,128,2048]{2,1,0:T(8,128)(2,1)S(1)}, bf16[2,128,2048]{2,1,0:T(8,128)(2,1)}, u32[]{:S(2)}) copy-start(bf16[2,128,2048]{2,1,0:T(8,128)(2,1)} %param.16) | copy-start | bytes 3145732
  (1 other events, 0.7 us)
Sparse Core Ops, SparseCore 0:
  8.9 42.3 all-gather.3
  57.3 36.2 all-gather.7
  95.1 36.9 all-gather.5
  226.7 69.8 reduce-scatter.1
where the time goes:
time: 549 us; the launch traced here: 543 us
  waiting for transfers between devices  225 us (41%)
  matrix products  118 us (21%)
  blocking collectives  82.9 us (15%)
  other arithmetic  50.8 us (9%)
  local copies, waits for them, and re-layouts  45.6 us (8%)
  between operations  13.4 us (2%)
  starting transfers between devices  6.59 us (1%)
    all_to_all x1, blocking collectives, device_step(): recv_buf = lax.all_to_all(send_buf, ('cp', 'tp'), 0, 0, tiled=True)  82.9 us
    all_to_all x1, waiting for transfers between devices, device_step(): lax.all_to_all(expert_out.reshape(experts * capacity, hidden), ('cp', 'tp...  77.6 us
    dot_general x12, matrix products, one_block(): jnp.einsum('qgrd,kgd->qgrk', q_blk, key_all, preferred_element_type=jnp.f...  44.5 us
    all_gather x1, waiting for transfers between devices, attention_residual(): gathered = lax.all_gather(hidden_in, 'tp', axis=0, tiled=True)  43.9 us
    reduce_scatter x1, waiting for transfers between devices, attention_residual(): reduced = lax.psum_scatter(part_sum, 'tp', scatter_dimension=0, tiled=True)  43 us
    all_gather x1, waiting for transfers between devices, attention_residual(): lax.all_gather(key_loc, 'cp', axis=0, tiled=True)  34.5 us
    all_gather x1, waiting for transfers between devices, attention_residual(): lax.all_gather(value_loc, 'cp', axis=0, tiled=True)  25.4 us
    dot_general x12, matrix products, one_block(): jnp.einsum('qgrk,kgd->qgrd', attn_prob, value_all, preferred_element_type...  18.4 us
  transfers between devices with their start and end apart: 5, of which 5 were waited for; matrix products, arithmetic and copies ran while one was open for 8% of the time, Pallas kernels for 0%

commit v1 on v0

--- a/solution.py
+++ b/solution.py
@@ -1,8 +1,13 @@
+import functools
 import math
 import jax
 import jax.numpy as jnp
 from jax import lax
+from jax.experimental import pallas as pl
+from jax.experimental.pallas import tpu as pltpu
 from jax.sharding import PartitionSpec as P
+
+MESH = pl.DeviceIdType.MESH
 
 
 def row_positions(row_ids, block_rows, cp_devs):
@@ -52,36 +57,216 @@
     return (hidden_in.astype(jnp.float32) + reduced).astype(jnp.bfloat16)
 
 
+def moe_kernel(dims, h_in, idx_ref, gate_ref, wg_hbm, wu_hbm, wd_hbm, y_ref,
+               wg, wu, wd, send, recv, ret, slots, gates, dmat, gmat, acc, hid,
+               wsem, ssem, rsem, bsem, csem):
+    n_cp, n_x, top_k, experts, cap, local_exp = dims
+    per_grp = 2 * n_x
+    rows = h_in.shape[0]
+    hidden = h_in.shape[1]
+    cp, tp = lax.axis_index('cp'), lax.axis_index('tp')
+    x_pos, core = tp // 2, tp % 2
+
+    def fwd(j, r):
+        dx, dc = r // 2, r % 2
+        return (cp + (dx + j) % n_cp) % n_cp, ((x_pos + dx) % n_x) * 2 + (core + dc) % 2
+
+    def back(j, r):
+        dx, dc = r // 2, r % 2
+        return (cp + n_cp - (dx + j) % n_cp) % n_cp, ((x_pos + n_x - dx) % n_x) * 2 + (core + dc) % 2
+
+    barrier = pltpu.get_barrier_semaphore()
+    for j in range(n_cp):
+        for r in range(per_grp):
+            if j or r:
+                c, t = fwd(j, r)
+                pl.semaphore_signal(barrier, inc=1, device_id={'cp': c, 'tp': t}, device_id_type=MESH)
+    loads = [pltpu.make_async_copy(wg_hbm, wg, wsem.at[0]), pltpu.make_async_copy(wu_hbm, wu, wsem.at[1]), pltpu.make_async_copy(wd_hbm, wd, wsem.at[2])]
+    for ld in loads:
+        ld.start()
+
+    e_iota = lax.broadcasted_iota(jnp.int32, (experts, rows), 0)
+    hit = jnp.zeros((experts, rows), jnp.float32)
+    gsel = jnp.zeros((experts, rows), jnp.float32)
+    for k in range(top_k):
+        m = idx_ref[k:k + 1, :] == e_iota
+        hit = hit + jnp.where(m, 1.0, 0.0)
+        gsel = gsel + jnp.where(m, gate_ref[k:k + 1, :], 0.0)
+    before = jnp.where(lax.broadcasted_iota(jnp.int32, (rows, rows), 0) < lax.broadcasted_iota(jnp.int32, (rows, rows), 1), 1.0, 0.0)
+    count = jnp.dot(hit.astype(jnp.bfloat16), before.astype(jnp.bfloat16), preferred_element_type=jnp.float32)
+    slots[...] = jnp.where(hit > 0.5, count, -1.0)
+    gates[...] = gsel
+    c_iota = lax.broadcasted_iota(jnp.int32, (cap, rows), 0).astype(jnp.float32)
+
+    def build(j, ref, gated):
+        for e in range(local_exp):
+            for r in range(per_grp):
+                c, t = fwd(j, r)
+                expert = (c * (2 * n_x) + t) * local_exp + e
+                eq = jnp.broadcast_to(slots[pl.ds(expert, 1), :], (cap, rows)) == c_iota
+                val = jnp.broadcast_to(gates[pl.ds(expert, 1), :], (cap, rows)) if gated else 1.0
+                ref[pl.ds((e * per_grp + r) * cap, cap), :] = jnp.where(eq, val, 0.0)
+
+    def dispatch(j, r):
+        c, t = fwd(j, r)
+        out = []
+        for e in range(local_exp):
+            if j == 0 and r == 0:
+                out.append(pltpu.make_async_copy(send.at[j, e * per_grp + r], recv.at[j, e * per_grp + r], rsem.at[j, e * per_grp + r]))
+            else:
+                out.append(pltpu.make_async_remote_copy(send.at[j, e * per_grp + r], recv.at[j, e * per_grp + r], ssem.at[j, e * per_grp + r], rsem.at[j, e * per_grp + r], device_id={'cp': c, 'tp': t}, device_id_type=MESH))
+        return out
+
+    def giveback(j, r):
+        c, t = back(j, r)
+        out = []
+        for e in range(local_exp):
+            if j == 0 and r == 0:
+                out.append(pltpu.make_async_copy(recv.at[j, e * per_grp + r], ret.at[j, e * per_grp + r], csem.at[j, e * per_grp + r]))
+            else:
+                out.append(pltpu.make_async_remote_copy(recv.at[j, e * per_grp + r], ret.at[j, e * per_grp + r], bsem.at[j, e * per_grp + r], csem.at[j, e * per_grp + r], device_id={'cp': c, 'tp': t}, device_id_type=MESH))
+        return out
+
+    grp_rows = local_exp * per_grp * cap
+    half = per_grp * cap
+    wide = 512
+    order = [r for r in range(per_grp) if r >= 2] + [1, 0]
+    for j in range(n_cp):
+        build(j, dmat, False)
+
+        def fill(n, carry, j=j):
+            cols = pl.ds(pl.multiple_of(n * wide, wide), wide)
+            picked = jnp.dot(dmat[...].astype(jnp.bfloat16), h_in[:, cols], preferred_element_type=jnp.float32).astype(jnp.bfloat16)
+            send[j, :, :, cols] = picked.reshape(local_exp * per_grp, cap, wide)
+            return carry
+
+        lax.fori_loop(0, hidden // wide, fill, 0)
+        if j == 0:
+            pl.semaphore_wait(barrier, n_cp * per_grp - 1)
+        for r in order:
+            for cpy in dispatch(j, r):
+                cpy.start()
+
+    def init(n, carry):
+        cols = pl.ds(pl.multiple_of(n * wide, wide), wide)
+        acc[:, cols] = h_in[:, cols].astype(jnp.float32)
+        return carry
+
+    lax.fori_loop(0, hidden // wide, init, 0)
+    for ld in loads:
+        ld.wait()
+    ffn = wg.shape[2]
+    for j in range(n_cp):
+        for r in order:
+            for cpy in dispatch(j, r):
+                if j == 0 and r == 0:
+                    cpy.wait()
+                else:
+                    cpy.wait_recv()
+        for e in range(local_exp):
+            def up(n, carry, j=j, e=e):
+                cols = pl.ds(pl.multiple_of(n * 256, 256), 256)
+                rows_in = recv[j, pl.ds(e * per_grp, per_grp)].reshape(half, hidden)
+                g = jnp.dot(rows_in, wg[e, :, cols], preferred_element_type=jnp.float32)
+                u = jnp.dot(rows_in, wu[e, :, cols], preferred_element_type=jnp.float32)
+                hid[:, cols] = (g * (1.0 / (1.0 + jnp.exp(-g))) * u).astype(jnp.bfloat16)
+                return carry
+
+            def down(n, carry, j=j, e=e):
+                cols = pl.ds(pl.multiple_of(n * wide, wide), wide)
+                z = jnp.dot(hid[...], wd[e, :, cols], preferred_element_type=jnp.float32).astype(jnp.bfloat16)
+                recv[j, pl.ds(e * per_grp, per_grp), :, cols] = z.reshape(per_grp, cap, wide)
+                return carry
+
+            lax.fori_loop(0, ffn // 256, up, 0)
+            lax.fori_loop(0, hidden // wide, down, 0)
+            for r in order:
+                giveback(j, r)[e].start()
+
+    for j in range(n_cp):
+        build(j, gmat, True)
+        for r in order:
+            for cpy in giveback(j, r):
+                if j == 0 and r == 0:
+                    cpy.wait()
+                else:
+                    cpy.wait_recv()
+
+        def comb(n, carry, j=j):
+            cols = pl.ds(pl.multiple_of(n * wide, wide), wide)
+            g0 = gmat[...]
+            hi = g0.astype(jnp.bfloat16)
+            g1 = g0 - hi.astype(jnp.float32)
+            mid = g1.astype(jnp.bfloat16)
+            lo = (g1 - mid.astype(jnp.float32)).astype(jnp.bfloat16)
+            z = ret[j, :, :, cols].reshape(grp_rows, wide)
+            dims_t = (((0,), (0,)), ((), ()))
+            tot = lax.dot_general(lo, z, dims_t, preferred_element_type=jnp.float32)
+            tot = tot + lax.dot_general(mid, z, dims_t, preferred_element_type=jnp.float32)
+            tot = tot + lax.dot_general(hi, z, dims_t, preferred_element_type=jnp.float32)
+            acc[:, cols] += tot
+            return carry
+
+        lax.fori_loop(0, hidden // wide, comb, 0)
+
+    def fin(n, carry):
+        cols = pl.ds(pl.multiple_of(n * wide, wide), wide)
+        y_ref[:, cols] = acc[:, cols].astype(jnp.bfloat16)
+        return carry
+
+    lax.fori_loop(0, hidden // wide, fin, 0)
+    for j in range(n_cp):
+        for r in range(per_grp):
+            if j or r:
+                for cpy in dispatch(j, r) + giveback(j, r):
+                    cpy.wait_send()
+
+
+def expert_layer(mesh, resid_h, expert_idx, gate_vals, w_gate, w_up, w_down):
+    n_cp, n_x = mesh.shape['cp'], mesh.shape['tp'] // 2
+    rows, hidden = resid_h.shape
+    top_k = expert_idx.shape[1]
+    local_exp, _, ffn = w_gate.shape
+    experts = local_exp * n_cp * n_x * 2
+    cap = rows * top_k // experts
+    slots = local_exp * 2 * n_x
+    dims = (n_cp, n_x, top_k, experts, cap, local_exp)
+    vm = pl.BlockSpec(memory_space=pltpu.VMEM)
+    hb = pl.BlockSpec(memory_space=pl.ANY)
+    sems = [pltpu.SemaphoreType.DMA((n_cp, slots)) for _ in range(4)]
+    return pl.pallas_call(
+        functools.partial(moe_kernel, dims),
+        out_shape=jax.ShapeDtypeStruct((rows, hidden), jnp.bfloat16),
+        in_specs=[vm, vm, vm, hb, hb, hb],
+        out_specs=vm,
+        scratch_shapes=[
+            pltpu.VMEM((local_exp, hidden, ffn), jnp.bfloat16),
+            pltpu.VMEM((local_exp, hidden, ffn), jnp.bfloat16),
+            pltpu.VMEM((local_exp, ffn, hidden), jnp.bfloat16),
+            pltpu.VMEM((n_cp, slots, cap, hidden), jnp.bfloat16),
+            pltpu.VMEM((n_cp, slots, cap, hidden), jnp.bfloat16),
+            pltpu.VMEM((n_cp, slots, cap, hidden), jnp.bfloat16),
+            pltpu.VMEM((experts, rows), jnp.float32),
+            pltpu.VMEM((experts, rows), jnp.float32),
+            pltpu.VMEM((slots * cap, rows), jnp.float32),
+            pltpu.VMEM((slots * cap, rows), jnp.float32),
+            pltpu.VMEM((rows, hidden), jnp.float32),
+            pltpu.VMEM((2 * n_x * cap, ffn), jnp.bfloat16),
+            pltpu.SemaphoreType.DMA((3,)),
+        ] + sems,
+        compiler_params=pltpu.CompilerParams(collective_id=1, has_side_effects=True, vmem_limit_bytes=64 * 1024 * 1024 - 65536),
+        name='moe',
+    )(resid_h, expert_idx.T, gate_vals.T, w_gate, w_up, w_down)
+
+
 def solution(mesh):
     cp_devs = mesh.shape['cp']
-    group_devs = cp_devs * mesh.shape['tp']
     row_spec = P(('dp', 'cp', 'tp'), None)
     head_spec = P(None, 'tp', None)
     expert_spec = P(('cp', 'tp'), None, None)
 
     def device_step(hidden_in, w_query, w_key, w_value, w_out, expert_idx, gate_vals, w_gate, w_up, w_down):
-        tok_dev, hidden = hidden_in.shape
-        top_k = expert_idx.shape[1]
-        local_exp = w_gate.shape[0]
-        experts = local_exp * group_devs
-        capacity = tok_dev * top_k // experts
         resid_h = attention_residual(hidden_in, w_query, w_key, w_value, w_out, cp_devs)
-        flat_idx = expert_idx.reshape(-1)
-        hit_mask = flat_idx[:, None] == jnp.arange(experts)[None, :]
-        slot_all = jnp.cumsum(hit_mask.astype(jnp.int32), axis=0) - 1
-        slot_ids = jnp.sum(jnp.where(hit_mask, slot_all, 0), axis=1)
-        dest_row = flat_idx * capacity + slot_ids
-        src_rows = jnp.zeros((experts * capacity,), jnp.int32).at[dest_row].set(jnp.arange(tok_dev * top_k, dtype=jnp.int32) // top_k)
-        send_buf = jnp.take(resid_h, src_rows, axis=0)
-        recv_buf = lax.all_to_all(send_buf, ('cp', 'tp'), 0, 0, tiled=True)
-        expert_in = recv_buf.reshape(group_devs, local_exp, capacity, hidden)
-        gate_act = jnp.einsum('gech,ehf->gecf', expert_in, w_gate, preferred_element_type=jnp.float32)
-        up_act = jnp.einsum('gech,ehf->gecf', expert_in, w_up, preferred_element_type=jnp.float32)
-        hidden_act = (jax.nn.silu(gate_act) * up_act).astype(jnp.bfloat16)
-        expert_out = jnp.einsum('gecf,efh->gech', hidden_act, w_down, preferred_element_type=jnp.float32).astype(jnp.bfloat16)
-        returned = lax.all_to_all(expert_out.reshape(experts * capacity, hidden), ('cp', 'tp'), 0, 0, tiled=True)
-        per_choice = jnp.take(returned, dest_row, axis=0).reshape(tok_dev, top_k, hidden)
-        moe_sum = jnp.sum(gate_vals[:, :, None] * per_choice, axis=1)
-        return (resid_h.astype(jnp.float32) + moe_sum).astype(jnp.bfloat16)
+        return expert_layer(mesh, resid_h, expert_idx, gate_vals, w_gate, w_up, w_down)
 
     return jax.shard_map(device_step, mesh=mesh, in_specs=(row_spec, head_spec, head_spec, head_spec, P('tp', None, None), row_spec, row_spec, expert_spec, expert_spec, expert_spec), out_specs=row_spec, check_vma=False)

time: 549 us -> 502 us (0.914)
  Pallas kernels: 0 us -> 195 us
  blocking collectives: 82.9 us -> 0 us
  matrix products: 118 us -> 62.5 us
  waiting for transfers between devices: 225 us -> 174 us
  other arithmetic: 50.8 us -> 21 us
  local copies, waits for them, and re-layouts: 45.6 us -> 28.9 us
  starting transfers between devices: 6.59 us -> 0.19 us
    pallas_call x0 -> x1, Pallas kernels: none -> 195 us  [expert_layer(): pl.pallas_call(functools.partial(moe_kernel, dims), out_shape=jax.ShapeDt...]
    all_to_all x1 -> x0, blocking collectives: 82.9 us -> none  [device_step(): recv_buf = lax.all_to_all(send_buf, ('cp', 'tp'), 0, 0, tiled=True)]
    all_to_all x1 -> x0, waiting for transfers between devices: 77.6 us -> none  [device_step(): lax.all_to_all(expert_out.reshape(experts * capacity, hidden), ('cp', 'tp...]
    dot_general x3 -> x0, matrix products: 32.4 us -> none  [the longest x1 10.9 us: device_step(): jnp.einsum('gech,ehf->gecf', expert_in, w_up, preferred_element_type=jnp....]
    reduce_scatter x1, waiting for transfers between devices: 43 us -> 70.1 us  [attention_residual(): reduced = lax.psum_scatter(part_sum, 'tp', scatter_dimension=0, tiled=True)]
    dot_general x12, matrix products: 44.5 us -> 20.3 us  [one_block(): jnp.einsum('qgrd,kgd->qgrk', q_blk, key_all, preferred_element_type=jnp.f...]
    gather x2 -> x0, local copies, waits for them, and re-layouts: 23.4 us -> none  [the longest x1 16.4 us: device_step(): jnp.take(returned, dest_row, axis=0).reshape(tok_dev, top_k, hidden)]
    another operation x2 -> x0, other arithmetic: 18.2 us -> none
  transfers between devices with their start and end apart: 5 -> 4, of which waited for: 5 -> 4; matrix products, arithmetic and copies ran while one was open for 8% -> 3% of each run, Pallas kernels for 0% -> 0%
where the time goes in v1:
time: 502 us; the launch traced here: 496 us
  Pallas kernels  195 us (39%)
  waiting for transfers between devices  174 us (35%)
  matrix products  62.5 us (12%)
  local copies, waits for them, and re-layouts  28.9 us (6%)
  other arithmetic  21 us (4%)
  between operations  13.2 us (3%)
    pallas_call x1, Pallas kernels, expert_layer(): pl.pallas_call(functools.partial(moe_kernel, dims), out_shape=jax.ShapeDt...  195 us
    reduce_scatter x1, waiting for transfers between devices, attention_residual(): reduced = lax.psum_scatter(part_sum, 'tp', scatter_dimension=0, tiled=True)  70.1 us
    all_gather x1, waiting for transfers between devices, attention_residual(): gathered = lax.all_gather(hidden_in, 'tp', axis=0, tiled=True)  43.9 us
    all_gather x1, waiting for transfers between devices, attention_residual(): lax.all_gather(key_loc, 'cp', axis=0, tiled=True)  34.5 us
    all_gather x1, waiting for transfers between devices, attention_residual(): lax.all_gather(value_loc, 'cp', axis=0, tiled=True)  24.8 us
    dot_general x12, matrix products, one_block(): jnp.einsum('qgrd,kgd->qgrk', q_blk, key_all, preferred_element_type=jnp.f...  20.3 us
    dot_general x12, matrix products, one_block(): jnp.einsum('qgrk,kgd->qgrd', attn_prob, value_all, preferred_element_type...  18.4 us
    reduce_sum x12, other arithmetic, one_block(): attn_prob = jax.nn.softmax(scores, axis=-1).astype(jnp.bfloat16)  12.2 us
  transfers between devices with their start and end apart: 4, of which 4 were waited for; matrix products, arithmetic and copies ran while one was open for 3% of the time, Pallas kernels for 0%

profile of v1, /device:TPU:97, one launch (start us, length us, event | category | flops | bytes accessed | tf_op | source)
XLA Modules:
  0.0 495.9 jit_solution(2429570224741782577)
XLA Ops:
  7.4 43.9 %all-gather.4.cloned.1.call-done = bf16[1536,2048]{1,0:T(8,128)(2,1)} async-done(((bf16[192,2048]{1,0:T(8,128)(2,1)}), bf16[1536,2048]{1,0:T(8,128)(2,1)}) %all-gather.4.cloned.1.call-update) | async-done | bytes 6291472 | tf_op jit(solution)/shard_map/all_gather | solution.py:44
  51.3 5.7 %convolution_convert_fusion = bf16[1536,256]{1,0:T(8,128)(2,1)} fusion(bf16[1536,2048]{1,0:T(8,128)(2,1)} %all-gather.4.cloned.1.call-done, bf16[256,8,2,128]{3,2,1,0:T(2,128)(2,1)} %bitcast.83), kind=kOutput, calls=%fused_computation.35 | convolution fusion | flops 1611005952 | bytes 8126464 | tf_op jit(solution)/shard_map/dot_general | solution.py:48
  57.2 5.6 %convolution_convert_fusion.1 = bf16[1536,256]{1,0:T(8,128)(2,1)} fusion(bf16[1536,2048]{1,0:T(8,128)(2,1)} %all-gather.4.cloned.1.call-done, bf16[256,8,2,128]{3,2,1,0:T(2,128)(2,1)S(1)} %bitcast.84), kind=kOutput, calls=%fused_computation.36 | convolution fusion | flops 1611005952 | bytes 8126464 | tf_op jit(solution)/shard_map/dot_general | solution.py:47
  63.0 4.6 convolution_convert_fusion.2
  68.7 24.8 %all-gather.8.cloned.1.call-done = bf16[6144,256]{1,0:T(8,128)(2,1)} async-done(((bf16[1536,256]{1,0:T(8,128)(2,1)}), bf16[6144,256]{1,0:T(8,128)(2,1)}) %all-gather.8.cloned.1.call-update) | async-done | bytes 3145744 | tf_op jit(solution)/shard_map/all_gather | solution.py:50
  93.5 4.1 copy_bitcast_fusion.2
  97.6 34.5 %all-gather.6.cloned.1.call-done = bf16[6144,256]{1,0:T(8,128)(2,1)} async-done(((bf16[1536,256]{1,0:T(8,128)(2,1)}), bf16[6144,256]{1,0:T(8,128)(2,1)}) %all-gather.6.cloned.1.call-update) | async-done | bytes 3145744 | tf_op jit(solution)/shard_map/all_gather | solution.py:49
  132.1 2.4 copy_bitcast_fusion.3
  134.5 77.1 %while.11 = (s32[]{:T(128)}, bf16[12,128,2,1,128]{4,2,1,0,3:T(2,128)(2,1)}, s32[12,128]{1,0:T(8,128)S(1)}, bf16[12,128,2,1,128]{4,2,1,0,3:T(2,128)(2,1)}, bf16[6...) while((s32[]{:T(128)}, bf16[12,128,2,1,128]{4,2,1,0,3:T(2,128)(2,1)}, ...), condition=%wide.region_3.4_spmd.clone, body=%wide.region_0.3_spmd.clone.sunk | while | flops 818830848 | bytes 39770748 | solution.py:35
  136.2 1.7 fusion.63
  142.6 1.7 fusion.63
  149.0 1.7 fusion.63
  155.4 1.7 fusion.63
  161.8 1.7 fusion.63
  168.2 1.7 fusion.63
  174.6 1.7 fusion.63
  193.9 1.7 fusion.63
  200.3 1.7 fusion.63
  206.7 1.7 fusion.63
  211.6 7.8 %fusion.32 = f32[1536,2048]{1,0:T(8,128)} fusion(bf16[256,2048]{1,0:T(8,128)(2,1)} %bitcast.79, bf16[192,8,2,128]{3,2,1,0:T(2,128)(2,1)} %bitcast.80), kind=kOutput, calls=%fused_computation.45 | convolution fusion | flops 1610612736 | bytes 14417920 | tf_op jit(solution)/shard_map/dot_general | solution.py:55
  219.5 70.1 %reduce-scatter.2.cloned.1.call-done = f32[192,2048]{1,0:T(8,128)} async-done(((f32[1536,2048]{1,0:T(8,128)}), f32[192,2048]{1,0:T(8,128)}) %reduce-scatter.2.cloned.1.call-update) | async-done | bytes 1572880 | tf_op jit(solution)/shard_map/reduce_scatter | solution.py:56
  289.6 2.5 add_convert_fusion.h_in
  292.0 195.2 %moe.1 = bf16[192,2048]{1,0:T(8,128)(2,1)} custom-call(bf16[192,2048]{1,0:T(8,128)(2,1)} %add_convert_fusion.h_in, s32[8,192]{1,0:T(8,128)} %bitcast.81, f32[8,192]{1,0:T(8,128)} %bitcast.82, bf16[2,2048,1024]{2,1,0:T(8,128)(2,1)} %wg_hbm.1, bf16[2,2048,1024]{2,1,0:T(8,128)(2,1)} %wu_hbm.1, bf16[2,1024,2048]{2,1,0:T(8,128)(2,1)} %wd_hbm.1), custom_call_target="tpu_custom_call" | custom-call | tf_op jit(solution)/shard_map/moe/pallas_call | solution.py:237
  487.3 2.1 copy.64
  (127 shorter events, 61.7 us)
Async XLA Ops:
  6.5 50.6 %copy-start.2 = (bf16[2048,2,128]{2,1,0:T(2,128)(2,1)S(1)}, bf16[2048,2,128]{2,1,0:T(2,128)(2,1)}, u32[]{:S(2)}) copy-start(bf16[2048,2,128]{2,1,0:T(2,128)(2,1)} %param.14) | copy-start | bytes 3145732
  6.5 44.8 %all-gather.4.cloned.1.call-start = ((), (), s32[]{:S(2)}) async-start(), calls=%async_computation.1 | async-start | bytes 7077888 | tf_op jit(solution)/shard_map/all_gather | solution.py:44
  7.3 86.2 %all-gather.8.cloned.1.call-start = ((), (), s32[]{:S(2)}) async-start(), calls=%async_computation.3 | async-start | bytes 3932160 | tf_op jit(solution)/shard_map/all_gather | solution.py:50
  57.1 6.0 %copy-start.3 = (bf16[2048,2,128]{2,1,0:T(2,128)(2,1)S(1)}, bf16[2048,2,128]{2,1,0:T(2,128)(2,1)}, u32[]{:S(2)}) copy-start(bf16[2048,2,128]{2,1,0:T(2,128)(2,1)} %param.13) | copy-start | bytes 3145732
  57.1 75.0 %all-gather.6.cloned.1.call-start = ((), (), s32[]{:S(2)}) async-start(), calls=%async_computation.2 | async-start | bytes 3932160 | tf_op jit(solution)/shard_map/all_gather | solution.py:49
  62.9 226.7 %reduce-scatter.2.cloned.1.call-start = ((), (), s32[]{:S(2)}) async-start(), calls=%async_computation.4 | async-start | bytes 14155776 | tf_op jit(solution)/shard_map/reduce_scatter | solution.py:56
  136.2 2.7 copy-start
  142.6 2.7 copy-start
  149.0 2.7 copy-start
  155.4 2.7 copy-start
  161.8 2.7 copy-start
  168.2 2.7 copy-start
  174.6 2.7 copy-start
  181.0 2.7 copy-start
  187.4 2.7 copy-start
  193.8 2.7 copy-start
  200.2 2.7 copy-start
  206.7 2.7 copy-start
  219.4 70.1 %copy-start.1 = (bf16[192,2048]{1,0:T(8,128)(2,1)S(1)}, bf16[192,2048]{1,0:T(8,128)(2,1)}, u32[]{:S(2)}) copy-start(bf16[192,2048]{1,0:T(8,128)(2,1)} %param.12) | copy-start | bytes 2359300
Sparse Core Ops, SparseCore 0:
  8.9 42.3 all-gather.3
  57.2 36.2 all-gather.7
  95.1 36.9 all-gather.5
  219.6 69.8 reduce-scatter.1

commit v2 on v1

v2 whole, which is shorter than its diff:
```python
import functools
import jax
import jax.numpy as jnp
from jax import lax
from jax.experimental import pallas as pl
from jax.experimental.pallas import tpu as pltpu
from jax.sharding import PartitionSpec as P

MESH = pl.DeviceIdType.MESH


def attn_kernel(dims, x_in, wqkv, wo, h_ref,
                xbuf, wall, snd, land, kvp, mask, osnd, oland, wfull,
                lsem, xs, xr, ws, wr, qs, qr, ks, kr, os_, orr, gs, gr, ps, pr):
    n_cp, n_x, hd = dims
    rows, hidden = x_in.shape
    half = rows // 2
    units = n_x // 2
    n_units = n_cp * n_x
    blk = units * rows
    bf, f32 = jnp.bfloat16, jnp.float32
    cp, tp = lax.axis_index('cp'), lax.axis_index('tp')
    x_pos, core = tp // 2, tp % 2
    head = x_pos * n_cp + cp
    nbr = lambda d: (x_pos + d + n_x) % n_x
    at_x = lambda xx: {'cp': cp, 'tp': xx * 2 + core}
    at_y = lambda yy: {'cp': yy, 'tp': tp}
    partner = {'cp': cp, 'tp': x_pos * 2 + 1 - core}

    def remote(src, dst, s_sem, r_sem, dev):
        return pltpu.make_async_remote_copy(src, dst, s_sem, r_sem, device_id=dev, device_id_type=MESH)

    def place(c, xx):
        hi = xx // units
        return (c * (1 - hi) + (2 * n_cp - 1 - c) * hi) * units + xx % units

    barrier = pltpu.get_barrier_semaphore()
    offs = [(dy, dx) for dy in range(n_cp) for dx in range(n_x) if dy or dx]
    for dy, dx in offs:
        pl.semaphore_signal(barrier, inc=1, device_id={'cp': (cp + dy) % n_cp, 'tp': nbr(dx) * 2 + core}, device_id_type=MESH)
    pl.semaphore_signal(barrier, inc=1, device_id=partner, device_id_type=MESH)
    load_w = pltpu.make_async_copy(wqkv, wall.at[core], lsem.at[0])
    load_o = pltpu.make_async_copy(wo, wfull.at[tp], lsem.at[1])
    load_w.start()
    load_o.start()
    pl.semaphore_wait(barrier, len(offs) + 1)

    parts = [pl.ds(0, half), pl.ds(half, half)]
    def x_own(d, p):
        slot = 0 if d == 1 else n_x - 2
        return remote(x_in.at[parts[p]], xbuf.at[slot, parts[p]], xs.at[slot, p], xr.at[slot, p], at_x(nbr(d)))

    def x_fwd(d):
        slot, p = (0, 0) if d == 1 else (n_x - 2, 1)
        return remote(xbuf.at[slot, parts[p]], xbuf.at[1, parts[p]], xs.at[1, p], xr.at[1, p], at_x(nbr(d)))

    for d, p in ((1, 0), (-1, 1), (1, 1), (-1, 0)):
        x_own(d, p).start()
    w_part = remote(wqkv, wall.at[core], gs.at[0], gr.at[0], partner)
    w_part.start()

    r_io = lax.broadcasted_iota(jnp.int32, (blk, blk), 0)
    c_io = lax.broadcasted_iota(jnp.int32, (blk, blk), 1)
    q_pos = r_io + jnp.where(r_io >= rows, rows, 0) + core * rows
    k_pos = c_io + jnp.where(c_io >= rows, rows, 0)
    mask[:, 0:blk] = jnp.where(k_pos + core * rows <= q_pos, 1.0, 0.0)
    mask[:, blk:] = jnp.where(k_pos + (1 - core) * rows <= q_pos, 1.0, 0.0)

    def q_send(s, dy):
        u = place(cp, nbr(-s))
        return remote(snd.at[s, dy - 1], land.at[u], qs.at[s, dy - 1], qr.at[s, dy - 1], at_y((cp + dy) % n_cp))

    def q_recv(s, dy):
        u = place((cp - dy + n_cp) % n_cp, nbr(-s))
        return remote(snd.at[s, dy - 1], land.at[u], qs.at[s, dy - 1], qr.at[s, dy - 1], at_y((cp + dy) % n_cp))

    def kv_send(s, dy):
        u = place((cp - dy + n_cp) % n_cp, nbr(-s))
        return remote(land.at[u, :, pl.ds(hd, 2 * hd)], kvp.at[u], ks.at[s, dy], kr.at[s, dy], partner)

    def project(s):
        for dy in (1, n_cp - 1, 2, 0):
            i = (cp + dy) % n_cp
            cols = pl.ds(pl.multiple_of((i % 2) * 3 * hd, 3 * hd), 3 * hd)
            xv = x_in[...] if s == 0 else xbuf[s - 1]
            res = jnp.dot(xv, wall[i // 2, :, cols], preferred_element_type=f32).astype(bf)
            if dy:
                snd[s, dy - 1] = res
                q_send(s, dy).start()
            else:
                land[place(cp, nbr(-s))] = res
                kv_send(s, 0).start()

    def relay(s):
        for dy in (1, n_cp - 1, 2):
            q_recv(s, dy).wait_recv()
            kv_send(s, dy).start()

    load_w.wait()
    w_part.wait()
    project(0)
    x_own(1, 0).wait_recv()
    x_fwd(1).start()
    x_own(-1, 1).wait_recv()
    x_fwd(-1).start()

    def w_own(d, p):
        slot = 0 if d == 1 else n_x - 2
        return remote(wfull.at[tp, w_parts[p]], wfull.at[tp, w_parts[p]], ws.at[slot, p], wr.at[slot, p], at_x(nbr(d)))

    def w_fwd(d):
        p = 0 if d == 1 else 1
        t = nbr(-d) * 2 + core
        return remote(wfull.at[t, w_parts[p]], wfull.at[t, w_parts[p]], ws.at[1, p], wr.at[1, p], at_x(nbr(d)))

    def w_pass(s):
        t = nbr(-s) * 2 + core
        return remote(wfull.at[t], wfull.at[t], ps.at[s], pr.at[s], partner)

    w_half = wo.shape[0] // 2
    w_parts = [pl.ds(0, w_half), pl.ds(w_half, w_half)]
    load_o.wait()
    for d, p in ((1, 0), (-1, 1), (1, 1), (-1, 0)):
        w_own(d, p).start()
    w_pass(0).start()

    x_own(1, 1).wait_recv()
    project(1)
    x_own(-1, 0).wait_recv()
    project(n_x - 1)
    relay(0)
    x_fwd(1).wait_recv()
    x_fwd(-1).wait_recv()
    project(2)
    for s in (1, n_x - 1, 2):
        relay(s)
    for s in range(n_x):
        for dy in range(n_cp):
            kv_send(s, dy).wait_recv()

    c_exp = hd ** -0.5 * 1.4426950408889634
    nt = (((1,), (1,)), ((), ()))

    def o_copy(b, u):
        hi = b // n_cp
        dst_cp = b * (1 - hi) + (2 * n_cp - 1 - b) * hi
        dst_x = hi * units + u
        cols = pl.ds(pl.multiple_of(head * hd, hd), hd)
        cpy = remote(osnd.at[b * units + u], oland.at[:, cols], os_.at[b * units + u], orr.at[head], {'cp': dst_cp, 'tp': dst_x * 2 + core})
        own = jnp.logical_and(dst_cp == cp, dst_x == x_pos)
        return cpy, own, cols

    def step(b, t, carry, masked):
        mx, den, acc = carry
        q = land[pl.ds(b * units, units), :, 0:hd].reshape(blk, hd)
        own_u = pl.ds(t * units, units)
        k1 = land[own_u, :, hd:2 * hd].reshape(blk, hd)
        k2 = kvp[own_u, :, 0:hd].reshape(blk, hd)
        s1 = lax.dot_general(q, k1, nt, preferred_element_type=f32)
        s2 = lax.dot_general(q, k2, nt, preferred_element_type=f32)
        if masked:
            s1 = jnp.where(mask[:, 0:blk] > 0.5, s1, -1e30)
            s2 = jnp.where(mask[:, blk:] > 0.5, s2, -1e30)
        top = jnp.maximum(jnp.max(s1, axis=1, keepdims=True), jnp.max(s2, axis=1, keepdims=True))
        new = jnp.maximum(mx, top)
        keep = jnp.exp2((mx - new) * c_exp)
        p1 = jnp.exp2((s1 - new) * c_exp)
        p2 = jnp.exp2((s2 - new) * c_exp)
        den = den * keep + jnp.sum(p1, axis=1, keepdims=True) + jnp.sum(p2, axis=1, keepdims=True)
        v1 = land[own_u, :, 2 * hd:3 * hd].reshape(blk, hd)
        v2 = kvp[own_u, :, hd:2 * hd].reshape(blk, hd)
        acc = acc * keep + jnp.dot(p1.astype(bf), v1, preferred_element_type=f32) + jnp.dot(p2.astype(bf), v2, preferred_element_type=f32)
        return new, den, acc

    def attend(b, carry):
        @pl.when(b == RELAY_AT)
        def _():
            for d, p in ((1, 0), (-1, 1)):
                w_own(d, p).wait_recv()
                w_fwd(d).start()
            for d, p in ((1, 1), (-1, 0)):
                w_own(d, p).wait_recv()
            w_pass(1).start()
            w_pass(n_x - 1).start()

        start = (jnp.full((blk, 1), -1e30, f32), jnp.zeros((blk, 1), f32), jnp.zeros((blk, hd), f32))
        start = step(b, b, start, True)
        mx, den, acc = lax.fori_loop(0, b, lambda t, c: step(b, t, c, False), start)
        o = (acc / den).astype(bf)
        for u in range(units):
            cpy, own, cols = o_copy(b, u)
            osnd[b * units + u] = o[u * rows:(u + 1) * rows]

            @pl.when(own)
            def _():
                oland[:, cols] = o[u * rows:(u + 1) * rows]

            @pl.when(jnp.logical_not(own))
            def _():
                cpy.start()
        return carry

    lax.fori_loop(0, 2 * n_cp, attend, 0)
    w_fwd(1).wait_recv()
    w_fwd(-1).wait_recv()
    w_pass(2).start()
    for dy, dx in offs:
        src = nbr(dx) * n_cp + (cp + dy) % n_cp
        cols = pl.ds(pl.multiple_of(src * hd, hd), hd)
        remote(osnd.at[0], oland.at[:, cols], os_.at[0], orr.at[src], partner).wait_recv()
    for s in range(n_x):
        w_pass(s).wait_recv()

    wide = 512
    def out(n, carry):
        cols = pl.ds(pl.multiple_of(n * wide, wide), wide)
        tot = jnp.dot(oland[...], wfull[:, :, cols].reshape(hidden_o, wide), preferred_element_type=f32)
        h_ref[:, cols] = (x_in[:, cols].astype(f32) + tot).astype(bf)
        return carry

    hidden_o = n_x * 2 * wo.shape[0]
    lax.fori_loop(0, hidden // wide, out, 0)

    for d, p in ((1, 0), (-1, 1), (1, 1), (-1, 0)):
        x_own(d, p).wait_send()
        w_own(d, p).wait_send()
    for d in (1, -1):
        x_fwd(d).wait_send()
        w_fwd(d).wait_send()
    for s in range(n_x):
        w_pass(s).wait_send()
        for dy in range(n_cp):
            kv_send(s, dy).wait_send()
            if dy:
                q_send(s, dy).wait_send()

    def drain(b, carry):
        for u in range(units):
            cpy, own, cols = o_copy(b, u)

            @pl.when(jnp.logical_not(own))
            def _():
                cpy.wait_send()
        return carry

    lax.fori_loop(0, 2 * n_cp, drain, 0)


RELAY_AT = 6


def attention_residual(mesh, hidden_in, w_query, w_key, w_value, w_out):
    n_cp, n_x = mesh.shape['cp'], mesh.shape['tp'] // 2
    rows, hidden = hidden_in.shape
    heads, hd = w_query.shape[1:]
    wqkv = jnp.stack([w_query, w_key, w_value], axis=2).reshape(hidden, heads * 3 * hd)
    wo = w_out.reshape(heads * hd, hidden)
    units = n_x // 2
    n_units = n_cp * n_x
    blk = units * rows
    bf = jnp.bfloat16
    dma = pltpu.SemaphoreType.DMA
    vm = pl.BlockSpec(memory_space=pltpu.VMEM)
    hb = pl.BlockSpec(memory_space=pl.ANY)
    return pl.pallas_call(
        functools.partial(attn_kernel, (n_cp, n_x, hd)),
        out_shape=jax.ShapeDtypeStruct((rows, hidden), bf),
        in_specs=[vm, hb, hb],
        out_specs=vm,
        scratch_shapes=[
            pltpu.VMEM((n_x - 1, rows, hidden), bf),
            pltpu.VMEM((2, hidden, heads * 3 * hd), bf),
            pltpu.VMEM((n_x, n_cp - 1, rows, 3 * hd), bf),
            pltpu.VMEM((n_units, rows, 3 * hd), bf),
            pltpu.VMEM((n_units, rows, 2 * hd), bf),
            pltpu.VMEM((blk, 2 * blk), jnp.float32),
            pltpu.VMEM((n_units, rows, hd), bf),
            pltpu.VMEM((rows, n_units * hd), bf),
            pltpu.VMEM((2 * n_x, heads * hd, hidden), bf),
            dma((2,)), dma((n_x - 1, 2)), dma((n_x - 1, 2)), dma((n_x - 1, 2)), dma((n_x - 1, 2)),
            dma((n_x, n_cp - 1)), dma((n_x, n_cp - 1)), dma((n_x, n_cp)), dma((n_x, n_cp)),
            dma((n_units,)), dma((n_units,)), dma((1,)), dma((1,)), dma((n_x,)), dma((n_x,)),
        ],
        compiler_params=pltpu.CompilerParams(collective_id=2, has_side_effects=True, vmem_limit_bytes=60 * 1024 * 1024),
        name='attn',
    )(hidden_in, wqkv, wo)


def moe_kernel(dims, h_in, idx_ref, gate_ref, wg_hbm, wu_hbm, wd_hbm, y_ref,
               wg, wu, wd, send, recv, ret, slots, gates, dmat, gmat, acc, hid,
               wsem, ssem, rsem, bsem, csem):
    n_cp, n_x, top_k, experts, cap, local_exp = dims
    per_grp = 2 * n_x
    rows = h_in.shape[0]
    hidden = h_in.shape[1]
    cp, tp = lax.axis_index('cp'), lax.axis_index('tp')
    x_pos, core = tp // 2, tp % 2

    chips = [(dy, dx) for dy in range(n_cp) for dx in range(n_x)]
    near = [(0, 1), (1, 0), (0, n_x - 1), (n_cp - 1, 0)]
    odd = [o for o in chips if o[0] % 2 and o[1] % 2]
    even = [o for o in chips if not (o[0] % 2 or o[1] % 2)][::-1]
    rest = [o for o in chips if o not in near + odd + even]
    plan = [[(dy, dx, dc) for dc in range(2) for dy, dx in g] for g in (near, odd, even, rest)]
    n_grp = len(plan)

    def fwd(j, r):
        dy, dx, dc = plan[j][r]
        return (cp + dy) % n_cp, ((x_pos + dx) % n_x) * 2 + (core + dc) % 2

    def back(j, r):
        dy, dx, dc = plan[j][r]
        return (cp + n_cp - dy) % n_cp, ((x_pos + n_x - dx) % n_x) * 2 + (core + dc) % 2

    def local(j, r):
        return plan[j][r] == (0, 0, 0)

    barrier = pltpu.get_barrier_semaphore()
    for j in range(n_grp):
        for r in range(per_grp):
            if not local(j, r):
                c, t = fwd(j, r)
                pl.semaphore_signal(barrier, inc=1, device_id={'cp': c, 'tp': t}, device_id_type=MESH)
    loads = [pltpu.make_async_copy(wg_hbm, wg, wsem.at[0]), pltpu.make_async_copy(wu_hbm, wu, wsem.at[1]), pltpu.make_async_copy(wd_hbm, wd, wsem.at[2])]
    for ld in loads:
        ld.start()

    e_iota = lax.broadcasted_iota(jnp.int32, (experts, rows), 0)
    hit = jnp.zeros((experts, rows), jnp.float32)
    gsel = jnp.zeros((experts, rows), jnp.float32)
    for k in range(top_k):
        m = idx_ref[k:k + 1, :] == e_iota
        hit = hit + jnp.where(m, 1.0, 0.0)
        gsel = gsel + jnp.where(m, gate_ref[k:k + 1, :], 0.0)
    before = jnp.where(lax.broadcasted_iota(jnp.int32, (rows, rows), 0) < lax.broadcasted_iota(jnp.int32, (rows, rows), 1), 1.0, 0.0)
    count = jnp.dot(hit.astype(jnp.bfloat16), before.astype(jnp.bfloat16), preferred_element_type=jnp.float32)
    slots[...] = jnp.where(hit > 0.5, count, -1.0)
    gates[...] = gsel
    c_iota = lax.broadcasted_iota(jnp.int32, (cap, rows), 0).astype(jnp.float32)

    def build(j, ref, gated):
        for e in range(local_exp):
            for r in range(per_grp):
                c, t = fwd(j, r)
                expert = (c * (2 * n_x) + t) * local_exp + e
                eq = jnp.broadcast_to(slots[pl.ds(expert, 1), :], (cap, rows)) == c_iota
                val = jnp.broadcast_to(gates[pl.ds(expert, 1), :], (cap, rows)) if gated else 1.0
                ref[pl.ds((e * per_grp + r) * cap, cap), :] = jnp.where(eq, val, 0.0)

    def dispatch(j, r, e):
        c, t = fwd(j, r)
        if local(j, r):
            return (pltpu.make_async_copy(send.at[j, e * per_grp + r], recv.at[j, e * per_grp + r], rsem.at[j, e * per_grp + r]))
        return (pltpu.make_async_remote_copy(send.at[j, e * per_grp + r], recv.at[j, e * per_grp + r], ssem.at[j, e * per_grp + r], rsem.at[j, e * per_grp + r], device_id={'cp': c, 'tp': t}, device_id_type=MESH))

    def giveback(j, r, e):
        c, t = back(j, r)
        if local(j, r):
            return (pltpu.make_async_copy(recv.at[j, e * per_grp + r], ret.at[j, e * per_grp + r], csem.at[j, e * per_grp + r]))
        return (pltpu.make_async_remote_copy(recv.at[j, e * per_grp + r], ret.at[j, e * per_grp + r], bsem.at[j, e * per_grp + r], csem.at[j, e * per_grp + r], device_id={'cp': c, 'tp': t}, device_id_type=MESH))

    grp_rows = local_exp * per_grp * cap
    half = per_grp * cap
    wide = 512
    order = range(per_grp)
    for j in range(n_grp):
        build(j, dmat, False)

        def fill(n, carry, j=j):
            cols = pl.ds(pl.multiple_of(n * wide, wide), wide)
            picked = jnp.dot(dmat[...].astype(jnp.bfloat16), h_in[:, cols], preferred_element_type=jnp.float32).astype(jnp.bfloat16)
            send[j, :, :, cols] = picked.reshape(local_exp * per_grp, cap, wide)
            return carry

        lax.fori_loop(0, hidden // wide, fill, 0)
        if j == 0:
            pl.semaphore_wait(barrier, n_cp * per_grp - 1)
        for e in range(local_exp):
            for r in order:
                dispatch(j, r, e).start()

    def init(n, carry):
        cols = pl.ds(pl.multiple_of(n * wide, wide), wide)
        acc[:, cols] = h_in[:, cols].astype(jnp.float32)
        return carry

    lax.fori_loop(0, hidden // wide, init, 0)
    for ld in loads:
        ld.wait()
    ffn = wg.shape[2]
    for j in range(n_grp):
        for e in range(local_exp):
            for r in order:
                if local(j, r):
                    dispatch(j, r, e).wait()
                else:
                    dispatch(j, r, e).wait_recv()

            def up(n, carry, j=j, e=e):
                cols = pl.ds(pl.multiple_of(n * 256, 256), 256)
                rows_in = recv[j, pl.ds(e * per_grp, per_grp)].reshape(half, hidden)
                g = jnp.dot(rows_in, wg[e, :, cols], preferred_element_type=jnp.float32)
                u = jnp.dot(rows_in, wu[e, :, cols], preferred_element_type=jnp.float32)
                hid[:, cols] = (g * (1.0 / (1.0 + jnp.exp(-g))) * u).astype(jnp.bfloat16)
                return carry

            def down(n, carry, j=j, e=e):
                cols = pl.ds(pl.multiple_of(n * wide, wide), wide)
                z = jnp.dot(hid[...], wd[e, :, cols], preferred_element_type=jnp.float32).astype(jnp.bfloat16)
                recv[j, pl.ds(e * per_grp, per_grp), :, cols] = z.reshape(per_grp, cap, wide)
                return carry

            lax.fori_loop(0, ffn // 256, up, 0)
            lax.fori_loop(0, hidden // wide, down, 0)
            for r in order:
                giveback(j, r, e).start()

    for j in range(n_grp):
        build(j, gmat, True)
        for e in range(local_exp):
            for r in order:
                if local(j, r):
                    giveback(j, r, e).wait()
                else:
                    giveback(j, r, e).wait_recv()

        def comb(n, carry, j=j):
            cols = pl.ds(pl.multiple_of(n * wide, wide), wide)
            g0 = gmat[...]
            hi = g0.astype(jnp.bfloat16)
            g1 = g0 - hi.astype(jnp.float32)
            mid = g1.astype(jnp.bfloat16)
            lo = (g1 - mid.astype(jnp.float32)).astype(jnp.bfloat16)
            z = ret[j, :, :, cols].reshape(grp_rows, wide)
            dims_t = (((0,), (0,)), ((), ()))
            tot = lax.dot_general(lo, z, dims_t, preferred_element_type=jnp.float32)
            tot = tot + lax.dot_general(mid, z, dims_t, preferred_element_type=jnp.float32)
            tot = tot + lax.dot_general(hi, z, dims_t, preferred_element_type=jnp.float32)
            acc[:, cols] += tot
            return carry

        lax.fori_loop(0, hidden // wide, comb, 0)

    def fin(n, carry):
        cols = pl.ds(pl.multiple_of(n * wide, wide), wide)
        y_ref[:, cols] = acc[:, cols].astype(jnp.bfloat16)
        return carry

    lax.fori_loop(0, hidden // wide, fin, 0)
    for j in range(n_grp):
        for r in range(per_grp):
            if not local(j, r):
                for e in range(local_exp):
                    dispatch(j, r, e).wait_send()
                    giveback(j, r, e).wait_send()


def expert_layer(mesh, resid_h, expert_idx, gate_vals, w_gate, w_up, w_down):
    n_cp, n_x = mesh.shape['cp'], mesh.shape['tp'] // 2
    rows, hidden = resid_h.shape
    top_k = expert_idx.shape[1]
    local_exp, _, ffn = w_gate.shape
    experts = local_exp * n_cp * n_x * 2
    cap = rows * top_k // experts
    slots = local_exp * 2 * n_x
    dims = (n_cp, n_x, top_k, experts, cap, local_exp)
    vm = pl.BlockSpec(memory_space=pltpu.VMEM)
    hb = pl.BlockSpec(memory_space=pl.ANY)
    sems = [pltpu.SemaphoreType.DMA((n_cp, slots)) for _ in range(4)]
    return pl.pallas_call(
        functools.partial(moe_kernel, dims),
        out_shape=jax.ShapeDtypeStruct((rows, hidden), jnp.bfloat16),
        in_specs=[vm, vm, vm, hb, hb, hb],
        out_specs=vm,
        scratch_shapes=[
            pltpu.VMEM((local_exp, hidden, ffn), jnp.bfloat16),
            pltpu.VMEM((local_exp, hidden, ffn), jnp.bfloat16),
            pltpu.VMEM((local_exp, ffn, hidden), jnp.bfloat16),
            pltpu.VMEM((n_cp, slots, cap, hidden), jnp.bfloat16),
            pltpu.VMEM((n_cp, slots, cap, hidden), jnp.bfloat16),
            pltpu.VMEM((n_cp, slots, cap, hidden), jnp.bfloat16),
            pltpu.VMEM((experts, rows), jnp.float32),
            pltpu.VMEM((experts, rows), jnp.float32),
            pltpu.VMEM((slots * cap, rows), jnp.float32),
            pltpu.VMEM((slots * cap, rows), jnp.float32),
            pltpu.VMEM((rows, hidden), jnp.float32),
            pltpu.VMEM((2 * n_x * cap, ffn), jnp.bfloat16),
            pltpu.SemaphoreType.DMA((3,)),
        ] + sems,
        compiler_params=pltpu.CompilerParams(collective_id=1, has_side_effects=True, vmem_limit_bytes=64 * 1024 * 1024 - 65536),
        name='moe',
    )(resid_h, expert_idx.T, gate_vals.T, w_gate, w_up, w_down)


def solution(mesh):
    row_spec = P(('dp', 'cp', 'tp'), None)
    head_spec = P(None, 'tp', None)
    expert_spec = P(('cp', 'tp'), None, None)

    def device_step(hidden_in, w_query, w_key, w_value, w_out, expert_idx, gate_vals, w_gate, w_up, w_down):
        resid_h = attention_residual(mesh, hidden_in, w_query, w_key, w_value, w_out)
        return expert_layer(mesh, resid_h, expert_idx, gate_vals, w_gate, w_up, w_down)

    return jax.shard_map(device_step, mesh=mesh, in_specs=(row_spec, head_spec, head_spec, head_spec, P('tp', None, None), row_spec, row_spec, expert_spec, expert_spec, expert_spec), out_specs=row_spec, check_vma=False)
```

time: 502 us -> 270 us (0.54); the launches traced: 496 us -> 270 us
  waiting for transfers between devices: 174 us -> 0 us
  matrix products: 62.5 us -> 0 us
  Pallas kernels: 195 us -> 253 us
  other arithmetic: 21 us -> 2.19 us
  local copies, waits for them, and re-layouts: 28.9 us -> 14.5 us
  between operations: 13.2 us -> 0.02 us
    all_gather x3 -> x0, waiting for transfers between devices: 103 us -> none  [the longest x1 43.9 us: attention_residual(): gathered = lax.all_gather(hidden_in, 'tp', axis=0, tiled=True)]
    pallas_call x0 -> x1, Pallas kernels: none -> 86.9 us  [attention_residual(): pl.pallas_call(functools.partial(attn_kernel, (n_cp, n_x, hd)), out_shape...]
    reduce_scatter x1 -> x0, waiting for transfers between devices: 70.1 us -> none  [attention_residual(): reduced = lax.psum_scatter(part_sum, 'tp', scatter_dimension=0, tiled=True)]
    dot_general x28 -> x0, matrix products: 62.5 us -> none  [the longest x12 20.3 us: one_block(): jnp.einsum('qgrd,kgd->qgrk', q_blk, key_all, preferred_element_type=jnp.f...]
    pallas_call x1, Pallas kernels: 195 us -> 166 us  [expert_layer(): pl.pallas_call(functools.partial(moe_kernel, dims), out_shape=jax.ShapeDt...]
    reduce_sum x12 -> x0, other arithmetic: 12.2 us -> none  [one_block(): attn_prob = jax.nn.softmax(scores, axis=-1).astype(jnp.bfloat16)]
    dynamic_slice x12 -> x0, local copies, waits for them, and re-layouts: 10.7 us -> none  [attend_blocks(): lax.map(one_block, (query_vecs.reshape(n_blocks, q_block, kv_heads, group...]
    dynamic_update_slice x12 -> x0, local copies, waits for them, and re-layouts: 8.44 us -> none  [attend_blocks(): lax.map(one_block, (query_vecs.reshape(n_blocks, q_block, kv_heads, group...]
  transfers between devices with their start and end apart: 4 -> 0, of which waited for: 4 -> 0; matrix products, arithmetic and copies ran while one was open for 3% -> 0% of each run, Pallas kernels for 0% -> 0%
where the time goes in v2:
time: 270 us
  Pallas kernels  253 us (94%)
  local copies, waits for them, and re-layouts  14.5 us (5%)
    pallas_call x1, Pallas kernels, expert_layer(): pl.pallas_call(functools.partial(moe_kernel, dims), out_shape=jax.ShapeDt...  166 us
    pallas_call x1, Pallas kernels, attention_residual(): pl.pallas_call(functools.partial(attn_kernel, (n_cp, n_x, hd)), out_shape...  86.9 us
    unnamed x6, local copies, waits for them, and re-layouts  11.7 us

profile of v2, /device:TPU:97, one launch (start us, length us, event | category | flops | bytes accessed | tf_op | source)
XLA Modules:
  0.0 269.7 jit_solution(7511136941856101167)
XLA Ops:
  0.0 0.0 copy-start
  0.0 3.8 %copy.12 = bf16[2048,2,128]{0,2,1:T(8,128)(2,1)} copy(bf16[2048,2,128]{2,1,0:T(2,128)(2,1)} %param.11) | data formatting | bytes 2097152 | tf_op args[1]
  3.8 3.7 %copy.13 = bf16[2048,2,128]{0,2,1:T(8,128)(2,1)} copy(bf16[2048,2,128]{2,1,0:T(2,128)(2,1)} %param.12) | data formatting | bytes 2097152 | tf_op args[2]
  7.5 0.0 copy-done
  7.5 2.1 copy.14
  9.6 2.2 pad_maximum_fusion
  11.8 2.8 %copy.15.wqkv = bf16[2048,768]{1,0:T(8,128)(2,1)} copy(bf16[2048,768]{0,1:T(8,128)(2,1)S(1)} %bitcast.7) | data formatting | bytes 6291456 | tf_op jit(solution)/shard_map/reshape | solution.py:256
  14.6 86.9 %attn.1.h_in = bf16[192,2048]{1,0:T(8,128)(2,1)} custom-call(bf16[192,2048]{1,0:T(8,128)(2,1)} %x_in.1, bf16[2048,768]{1,0:T(8,128)(2,1)} %copy.15.wqkv, bf16[256,2048]{1,0:T(8,128)(2,1)} %bitcast.11), custom_call_target="tpu_custom_call" | custom-call | tf_op jit(solution)/shard_map/attn/pallas_call | solution.py:265
  101.5 166.1 %moe.1 = bf16[192,2048]{1,0:T(8,128)(2,1)} custom-call(bf16[192,2048]{1,0:T(8,128)(2,1)} %attn.1.h_in, s32[8,192]{1,0:T(8,128)} %bitcast.12, f32[8,192]{1,0:T(8,128)} %bitcast.13, bf16[2,2048,1024]{2,1,0:T(8,128)(2,1)} %wg_hbm.1, bf16[2,2048,1024]{2,1,0:T(8,128)(2,1)} %wu_hbm.1, bf16[2,1024,2048]{2,1,0:T(8,128)(2,1)} %wd_hbm.1), custom_call_target="tpu_custom_call" | custom-call | tf_op jit(solution)/shard_map/moe/pallas_call | solution.py:470
  267.6 2.1 copy.17
Async XLA Ops:
  0.0 7.5 %copy-start = (bf16[2048,2,128]{2,1,0:T(2,128)(2,1)S(1)}, bf16[2048,2,128]{2,1,0:T(2,128)(2,1)}, u32[]{:S(2)}) copy-start(bf16[2048,2,128]{2,1,0:T(2,128)(2,1)} %param.13) | copy-start | bytes 3145732

commit v3 on v2

--- a/solution.py
+++ b/solution.py
@@ -9,9 +9,9 @@
 MESH = pl.DeviceIdType.MESH
 
 
-def attn_kernel(dims, x_in, wqkv, wo, h_ref,
-                xbuf, wall, snd, land, kvp, mask, osnd, oland, wfull,
-                lsem, xs, xr, ws, wr, qs, qr, ks, kr, os_, orr, gs, gr, ps, pr):
+def attn_kernel(dims, x_in, wq, wk, wv, wo, h_ref,
+                stage, pair, xbuf, wall, snd, land, kvp, vt, mask, osnd, oland, wfull,
+                lsem, xs, xr, ws, wr, qs, qr, ks, kr, os_, orr, gs, gr, ps, pr, ys, yr):
     n_cp, n_x, hd = dims
     rows, hidden = x_in.shape
     half = rows // 2
@@ -39,9 +39,10 @@
     for dy, dx in offs:
         pl.semaphore_signal(barrier, inc=1, device_id={'cp': (cp + dy) % n_cp, 'tp': nbr(dx) * 2 + core}, device_id_type=MESH)
     pl.semaphore_signal(barrier, inc=1, device_id=partner, device_id_type=MESH)
-    load_w = pltpu.make_async_copy(wqkv, wall.at[core], lsem.at[0])
-    load_o = pltpu.make_async_copy(wo, wfull.at[tp], lsem.at[1])
-    load_w.start()
+    loads = [pltpu.make_async_copy(w, stage.at[m], lsem.at[m + 1]) for m, w in enumerate((wq, wk, wv))]
+    load_o = pltpu.make_async_copy(wo, wfull.at[tp], lsem.at[0])
+    for ld in loads:
+        ld.start()
     load_o.start()
     pl.semaphore_wait(barrier, len(offs) + 1)
 
@@ -56,15 +57,28 @@
 
     for d, p in ((1, 0), (-1, 1), (1, 1), (-1, 0)):
         x_own(d, p).start()
-    w_part = remote(wqkv, wall.at[core], gs.at[0], gr.at[0], partner)
+    w_part = remote(wall.at[core], wall.at[core], gs.at[0], gr.at[0], partner)
+    heads = wall.shape[2] // (3 * hd)
+    rows_d = pair.shape[0] // heads
+    for ld in loads:
+        ld.wait()
+
+    def unpack(n, carry):
+        for m in range(3):
+            pair[...] = stage[m, pl.ds(pl.multiple_of(n * rows_d * heads, rows_d * heads), rows_d * heads), :].astype(f32)
+            for i in range(heads):
+                wall[core, pl.ds(pl.multiple_of(n * rows_d, rows_d), rows_d), (i * 3 + m) * hd:(i * 3 + m + 1) * hd] = pair[pl.ds(i, rows_d, stride=heads), :].astype(bf)
+        return carry
+
+    lax.fori_loop(0, hidden // rows_d, unpack, 0)
     w_part.start()
 
     r_io = lax.broadcasted_iota(jnp.int32, (blk, blk), 0)
     c_io = lax.broadcasted_iota(jnp.int32, (blk, blk), 1)
-    q_pos = r_io + jnp.where(r_io >= rows, rows, 0) + core * rows
-    k_pos = c_io + jnp.where(c_io >= rows, rows, 0)
-    mask[:, 0:blk] = jnp.where(k_pos + core * rows <= q_pos, 1.0, 0.0)
-    mask[:, blk:] = jnp.where(k_pos + (1 - core) * rows <= q_pos, 1.0, 0.0)
+    q_pos = c_io + jnp.where(c_io >= rows, rows, 0) + core * rows
+    k_pos = r_io + jnp.where(r_io >= rows, rows, 0)
+    mask[0:blk, :] = jnp.where(k_pos + core * rows <= q_pos, 1.0, 0.0)
+    mask[blk:, :] = jnp.where(k_pos + (1 - core) * rows <= q_pos, 1.0, 0.0)
 
     def q_send(s, dy):
         u = place(cp, nbr(-s))
@@ -96,33 +110,82 @@
             q_recv(s, dy).wait_recv()
             kv_send(s, dy).start()
 
-    load_w.wait()
-    w_part.wait()
-    project(0)
     x_own(1, 0).wait_recv()
     x_fwd(1).start()
     x_own(-1, 1).wait_recv()
     x_fwd(-1).start()
+    w_part.wait_recv()
+    project(0)
+
+    w_mid = wo.shape[0] // 2
+    w_qtr = w_mid // n_cp
+    w_cut = w_mid * 5 // 8
+    tp_at = lambda s: nbr(-s) * 2 + core
+
+    def w_rows(p, y):
+        if p == 0:
+            return pl.ds(0, w_cut)
+        if p == 1:
+            return pl.ds(w_cut, w_mid - w_cut)
+        return pl.ds(pl.multiple_of(w_mid + y * w_qtr, w_qtr), w_qtr)
 
     def w_own(d, p):
         slot = 0 if d == 1 else n_x - 2
-        return remote(wfull.at[tp, w_parts[p]], wfull.at[tp, w_parts[p]], ws.at[slot, p], wr.at[slot, p], at_x(nbr(d)))
-
-    def w_fwd(d):
-        p = 0 if d == 1 else 1
-        t = nbr(-d) * 2 + core
-        return remote(wfull.at[t, w_parts[p]], wfull.at[t, w_parts[p]], ws.at[1, p], wr.at[1, p], at_x(nbr(d)))
-
-    def w_pass(s):
-        t = nbr(-s) * 2 + core
-        return remote(wfull.at[t], wfull.at[t], ps.at[s], pr.at[s], partner)
-
-    w_half = wo.shape[0] // 2
-    w_parts = [pl.ds(0, w_half), pl.ds(w_half, w_half)]
+        blk_ref = wfull.at[tp, w_rows(p, cp)]
+        return remote(blk_ref, blk_ref, ws.at[slot, p], wr.at[slot, p], at_x(nbr(d)))
+
+    def w_fwd(d, p):
+        blk_ref = wfull.at[nbr(-d) * 2 + core, w_rows(p, cp)]
+        return remote(blk_ref, blk_ref, ws.at[1, p], wr.at[1, p], at_x(nbr(d)))
+
+    def w_share(s, dy):
+        blk_ref = wfull.at[tp_at(s), w_rows(2, cp)]
+        return remote(blk_ref, blk_ref, ys.at[s - 1, dy - 1], yr.at[s - 1, dy - 1], at_y((cp + dy) % n_cp))
+
+    def w_pass(s, p):
+        blk_ref = wfull.at[tp_at(s), pl.ds(p * w_mid, w_mid)]
+        return remote(blk_ref, blk_ref, ps.at[s, p], pr.at[s, p], partner)
+
+    relays = ((1, 0), (-1, 1), (-1, 2))
+    own_sends = ((1, 0), (-1, 1), (-1, 2), (1, 1), (-1, 0), (1, 2))
+    y_offs = (1, n_cp - 1, 2)
+
+    def w_step1():
+        for d, p in relays:
+            w_own(d, p).wait_recv()
+            w_fwd(d, p).start()
+        w_own(1, 2).wait_recv()
+        for dy in y_offs:
+            w_share(1, dy).start()
+            w_share(n_x - 1, dy).start()
+        w_own(1, 1).wait_recv()
+        w_own(-1, 0).wait_recv()
+        w_pass(1, 0).start()
+        w_pass(n_x - 1, 0).start()
+
+    def w_step2():
+        for d, p in relays[::-1]:
+            w_fwd(d, p).wait_recv()
+        for dy in y_offs:
+            w_share(2, dy).start()
+        w_pass(2, 0).start()
+
+    def w_step3():
+        for s in (1, n_x - 1):
+            for dy in y_offs:
+                w_share(s, dy).wait_recv()
+            w_pass(s, 1).start()
+
+    def w_step4():
+        for dy in y_offs:
+            w_share(2, dy).wait_recv()
+        w_pass(2, 1).start()
+
     load_o.wait()
-    for d, p in ((1, 0), (-1, 1), (1, 1), (-1, 0)):
+    for d, p in own_sends:
         w_own(d, p).start()
-    w_pass(0).start()
+    for p in range(2):
+        w_pass(0, p).start()
 
     x_own(1, 1).wait_recv()
     project(1)
@@ -150,43 +213,44 @@
         own = jnp.logical_and(dst_cp == cp, dst_x == x_pos)
         return cpy, own, cols
 
+    def flip(b, carry):
+        own_u = pl.ds(b * units, units)
+        cols = pl.ds(pl.multiple_of(b * blk, blk), blk)
+        vt[0, :, cols] = land[own_u, :, 2 * hd:3 * hd].reshape(blk, hd).T
+        vt[1, :, cols] = kvp[own_u, :, hd:2 * hd].reshape(blk, hd).T
+        return carry
+
+    lax.fori_loop(0, 2 * n_cp, flip, 0)
+
     def step(b, t, carry, masked):
         mx, den, acc = carry
         q = land[pl.ds(b * units, units), :, 0:hd].reshape(blk, hd)
         own_u = pl.ds(t * units, units)
+        cols = pl.ds(pl.multiple_of(t * blk, blk), blk)
         k1 = land[own_u, :, hd:2 * hd].reshape(blk, hd)
         k2 = kvp[own_u, :, 0:hd].reshape(blk, hd)
-        s1 = lax.dot_general(q, k1, nt, preferred_element_type=f32)
-        s2 = lax.dot_general(q, k2, nt, preferred_element_type=f32)
+        s1 = lax.dot_general(k1, q, nt, preferred_element_type=f32)
+        s2 = lax.dot_general(k2, q, nt, preferred_element_type=f32)
         if masked:
-            s1 = jnp.where(mask[:, 0:blk] > 0.5, s1, -1e30)
-            s2 = jnp.where(mask[:, blk:] > 0.5, s2, -1e30)
-        top = jnp.maximum(jnp.max(s1, axis=1, keepdims=True), jnp.max(s2, axis=1, keepdims=True))
+            s1 = jnp.where(mask[0:blk, :] > 0.5, s1, -1e30)
+            s2 = jnp.where(mask[blk:, :] > 0.5, s2, -1e30)
+        top = jnp.maximum(jnp.max(s1, axis=0, keepdims=True), jnp.max(s2, axis=0, keepdims=True))
         new = jnp.maximum(mx, top)
         keep = jnp.exp2((mx - new) * c_exp)
         p1 = jnp.exp2((s1 - new) * c_exp)
         p2 = jnp.exp2((s2 - new) * c_exp)
-        den = den * keep + jnp.sum(p1, axis=1, keepdims=True) + jnp.sum(p2, axis=1, keepdims=True)
-        v1 = land[own_u, :, 2 * hd:3 * hd].reshape(blk, hd)
-        v2 = kvp[own_u, :, hd:2 * hd].reshape(blk, hd)
-        acc = acc * keep + jnp.dot(p1.astype(bf), v1, preferred_element_type=f32) + jnp.dot(p2.astype(bf), v2, preferred_element_type=f32)
+        den = den * keep + jnp.sum(p1, axis=0, keepdims=True) + jnp.sum(p2, axis=0, keepdims=True)
+        acc = acc * keep + jnp.dot(vt[0, :, cols], p1.astype(bf), preferred_element_type=f32) + jnp.dot(vt[1, :, cols], p2.astype(bf), preferred_element_type=f32)
         return new, den, acc
 
     def attend(b, carry):
-        @pl.when(b == RELAY_AT)
-        def _():
-            for d, p in ((1, 0), (-1, 1)):
-                w_own(d, p).wait_recv()
-                w_fwd(d).start()
-            for d, p in ((1, 1), (-1, 0)):
-                w_own(d, p).wait_recv()
-            w_pass(1).start()
-            w_pass(n_x - 1).start()
-
-        start = (jnp.full((blk, 1), -1e30, f32), jnp.zeros((blk, 1), f32), jnp.zeros((blk, hd), f32))
+        for at, todo in zip(RELAY_AT, (w_step1, w_step2, w_step3)):
+            pl.when(b == at)(todo)
+
+        start = (jnp.full((1, blk), -1e30, f32), jnp.zeros((1, blk), f32), jnp.zeros((hd, blk), f32))
         start = step(b, b, start, True)
         mx, den, acc = lax.fori_loop(0, b, lambda t, c: step(b, t, c, False), start)
-        o = (acc / den).astype(bf)
+        o = (acc / den).T.astype(bf)
         for u in range(units):
             cpy, own, cols = o_copy(b, u)
             osnd[b * units + u] = o[u * rows:(u + 1) * rows]
@@ -201,15 +265,14 @@
         return carry
 
     lax.fori_loop(0, 2 * n_cp, attend, 0)
-    w_fwd(1).wait_recv()
-    w_fwd(-1).wait_recv()
-    w_pass(2).start()
+    w_step4()
     for dy, dx in offs:
         src = nbr(dx) * n_cp + (cp + dy) % n_cp
         cols = pl.ds(pl.multiple_of(src * hd, hd), hd)
         remote(osnd.at[0], oland.at[:, cols], os_.at[0], orr.at[src], partner).wait_recv()
     for s in range(n_x):
-        w_pass(s).wait_recv()
+        for p in range(2):
+            w_pass(s, p).wait_recv()
 
     wide = 512
     def out(n, carry):
@@ -223,12 +286,19 @@
 
     for d, p in ((1, 0), (-1, 1), (1, 1), (-1, 0)):
         x_own(d, p).wait_send()
+    for d, p in own_sends:
         w_own(d, p).wait_send()
+    for d, p in relays:
+        w_fwd(d, p).wait_send()
     for d in (1, -1):
         x_fwd(d).wait_send()
-        w_fwd(d).wait_send()
+    w_part.wait_send()
     for s in range(n_x):
-        w_pass(s).wait_send()
+        for p in range(2):
+            w_pass(s, p).wait_send()
+        for dy in y_offs:
+            if s:
+                w_share(s, dy).wait_send()
         for dy in range(n_cp):
             kv_send(s, dy).wait_send()
             if dy:
@@ -246,14 +316,14 @@
     lax.fori_loop(0, 2 * n_cp, drain, 0)
 
 
-RELAY_AT = 6
+RELAY_AT = (3, 5, 7)
 
 
 def attention_residual(mesh, hidden_in, w_query, w_key, w_value, w_out):
     n_cp, n_x = mesh.shape['cp'], mesh.shape['tp'] // 2
     rows, hidden = hidden_in.shape
     heads, hd = w_query.shape[1:]
-    wqkv = jnp.stack([w_query, w_key, w_value], axis=2).reshape(hidden, heads * 3 * hd)
+    wq, wk, wv = (w.reshape(hidden * heads, hd) for w in (w_query, w_key, w_value))
     wo = w_out.reshape(heads * hd, hidden)
     units = n_x // 2
     n_units = n_cp * n_x
@@ -265,30 +335,34 @@
     return pl.pallas_call(
         functools.partial(attn_kernel, (n_cp, n_x, hd)),
         out_shape=jax.ShapeDtypeStruct((rows, hidden), bf),
-        in_specs=[vm, hb, hb],
+        in_specs=[vm, hb, hb, hb, hb],
         out_specs=vm,
         scratch_shapes=[
+            pltpu.VMEM((3, heads * hidden, hd), bf),
+            pltpu.VMEM((heads * 256, hd), jnp.float32),
             pltpu.VMEM((n_x - 1, rows, hidden), bf),
             pltpu.VMEM((2, hidden, heads * 3 * hd), bf),
             pltpu.VMEM((n_x, n_cp - 1, rows, 3 * hd), bf),
             pltpu.VMEM((n_units, rows, 3 * hd), bf),
             pltpu.VMEM((n_units, rows, 2 * hd), bf),
-            pltpu.VMEM((blk, 2 * blk), jnp.float32),
+            pltpu.VMEM((2, hd, n_units * rows), bf),
+            pltpu.VMEM((2 * blk, blk), jnp.float32),
             pltpu.VMEM((n_units, rows, hd), bf),
             pltpu.VMEM((rows, n_units * hd), bf),
             pltpu.VMEM((2 * n_x, heads * hd, hidden), bf),
-            dma((2,)), dma((n_x - 1, 2)), dma((n_x - 1, 2)), dma((n_x - 1, 2)), dma((n_x - 1, 2)),
+            dma((4,)), dma((n_x - 1, 2)), dma((n_x - 1, 2)), dma((n_x - 1, 3)), dma((n_x - 1, 3)),
             dma((n_x, n_cp - 1)), dma((n_x, n_cp - 1)), dma((n_x, n_cp)), dma((n_x, n_cp)),
-            dma((n_units,)), dma((n_units,)), dma((1,)), dma((1,)), dma((n_x,)), dma((n_x,)),
+            dma((n_units,)), dma((n_units,)), dma((1,)), dma((1,)), dma((n_x, 2)), dma((n_x, 2)),
+            dma((n_x - 1, n_cp - 1)), dma((n_x - 1, n_cp - 1)),
         ],
         compiler_params=pltpu.CompilerParams(collective_id=2, has_side_effects=True, vmem_limit_bytes=60 * 1024 * 1024),
         name='attn',
-    )(hidden_in, wqkv, wo)
+    )(hidden_in, wq, wk, wv, wo)
 
 
 def moe_kernel(dims, h_in, idx_ref, gate_ref, wg_hbm, wu_hbm, wd_hbm, y_ref,
-               wg, wu, wd, send, recv, ret, slots, gates, dmat, gmat, acc, hid,
-               wsem, ssem, rsem, bsem, csem):
+               wg, wu, wd, send, recv, ret, slots, gates, tabs, held, dmat, gmat, acc, hid,
+               wsem, ssem, rsem, bsem, csem, tsem, tgot, hsem, hgot):
     n_cp, n_x, top_k, experts, cap, local_exp = dims
     per_grp = 2 * n_x
     rows = h_in.shape[0]
@@ -338,20 +412,67 @@
     gates[...] = gsel
     c_iota = lax.broadcasted_iota(jnp.int32, (cap, rows), 0).astype(jnp.float32)
 
-    def build(j, ref, gated):
+    def build(j, ref):
         for e in range(local_exp):
             for r in range(per_grp):
                 c, t = fwd(j, r)
                 expert = (c * (2 * n_x) + t) * local_exp + e
                 eq = jnp.broadcast_to(slots[pl.ds(expert, 1), :], (cap, rows)) == c_iota
-                val = jnp.broadcast_to(gates[pl.ds(expert, 1), :], (cap, rows)) if gated else 1.0
+                val = jnp.broadcast_to(gates[pl.ds(expert, 1), :], (cap, rows))
                 ref[pl.ds((e * per_grp + r) * cap, cap), :] = jnp.where(eq, val, 0.0)
 
-    def dispatch(j, r, e):
-        c, t = fwd(j, r)
-        if local(j, r):
-            return (pltpu.make_async_copy(send.at[j, e * per_grp + r], recv.at[j, e * per_grp + r], rsem.at[j, e * per_grp + r]))
-        return (pltpu.make_async_remote_copy(send.at[j, e * per_grp + r], recv.at[j, e * per_grp + r], ssem.at[j, e * per_grp + r], rsem.at[j, e * per_grp + r], device_id={'cp': c, 'tp': t}, device_id_type=MESH))
+    steps = (0, 1, n_x - 1, 2)
+    where_is = {plan[j][r]: (j, r) for j in range(n_grp) for r in range(per_grp)}
+    mid = hidden // 2
+    cols_of = (pl.ds(0, mid), pl.ds(mid, mid))
+
+    def peer(axis, d, dc):
+        if axis == 0:
+            return cp, ((x_pos + d) % n_x) * 2 + (core + dc) % 2
+        return (cp + d) % n_cp, x_pos * 2 + (core + dc) % 2
+
+    def table(axis, d):
+        c, t = peer(axis, d, 0)
+        return pltpu.make_async_remote_copy(slots, tabs.at[axis, d - 1], tsem.at[axis, d - 1], tgot.at[axis, d - 1], device_id={'cp': c, 'tp': t}, device_id_type=MESH)
+
+    def spread(axis, d):
+        c, t = peer(axis, d, 0)
+        return pltpu.make_async_remote_copy(h_in.at[:, cols_of[axis]], held.at[axis, d - 1], hsem.at[axis, d - 1], hgot.at[axis, d - 1], device_id={'cp': c, 'tp': t}, device_id_type=MESH)
+
+    def piece(axis, s, d, dc, e):
+        c, t = peer(1 - axis, d, dc)
+        k = e * per_grp + d * 2 + dc
+        j, r = where_is[(d, s, dc) if axis == 0 else (s, d, dc)]
+        src, dst = send.at[axis, s, k], recv.at[j, e * per_grp + r, :, cols_of[axis]]
+        got = rsem.at[axis, j, e * per_grp + r]
+        if d == 0 and dc == 0:
+            return pltpu.make_async_copy(src, dst, got)
+        return pltpu.make_async_remote_copy(src, dst, ssem.at[axis, s, k], got, device_id={'cp': c, 'tp': t}, device_id_type=MESH)
+
+    def pieces():
+        return [(axis, d, dc, e) for e in range(local_exp) for dc in range(2) for d in steps for axis in range(2)]
+
+    def select(axis, s):
+        tab = slots if s == 0 else tabs.at[axis, s - 1]
+        for d in range(n_x):
+            for dc in range(2):
+                c, t = peer(1 - axis, d, dc)
+                for e in range(local_exp):
+                    expert = (c * (2 * n_x) + t) * local_exp + e
+                    eq = jnp.broadcast_to(tab[pl.ds(expert, 1), :], (cap, rows)) == c_iota
+                    dmat[pl.ds((e * per_grp + d * 2 + dc) * cap, cap), :] = jnp.where(eq, 1.0, 0.0)
+
+        def fill(n, carry):
+            cols = pl.ds(pl.multiple_of(n * wide, wide), wide)
+            if s == 0:
+                from_h = h_in[:, pl.ds(pl.multiple_of(axis * mid + n * wide, wide), wide)]
+            else:
+                from_h = held[axis, s - 1, :, cols]
+            picked = jnp.dot(dmat[...].astype(jnp.bfloat16), from_h, preferred_element_type=jnp.float32).astype(jnp.bfloat16)
+            send[axis, s, :, :, cols] = picked.reshape(local_exp * per_grp, cap, wide)
+            return carry
+
+        lax.fori_loop(0, mid // wide, fill, 0)
 
     def giveback(j, r, e):
         c, t = back(j, r)
@@ -363,21 +484,24 @@
     half = per_grp * cap
     wide = 512
     order = range(per_grp)
-    for j in range(n_grp):
-        build(j, dmat, False)
-
-        def fill(n, carry, j=j):
-            cols = pl.ds(pl.multiple_of(n * wide, wide), wide)
-            picked = jnp.dot(dmat[...].astype(jnp.bfloat16), h_in[:, cols], preferred_element_type=jnp.float32).astype(jnp.bfloat16)
-            send[j, :, :, cols] = picked.reshape(local_exp * per_grp, cap, wide)
-            return carry
-
-        lax.fori_loop(0, hidden // wide, fill, 0)
-        if j == 0:
-            pl.semaphore_wait(barrier, n_cp * per_grp - 1)
-        for e in range(local_exp):
-            for r in order:
-                dispatch(j, r, e).start()
+    for axis in range(2):
+        select(axis, 0)
+    pl.semaphore_wait(barrier, n_grp * per_grp - 1)
+    for d in steps[1:]:
+        for axis in range(2):
+            table(axis, d).start()
+    for d in steps[1:]:
+        for axis in range(2):
+            spread(axis, d).start()
+    for axis, d, dc, e in pieces():
+        piece(axis, 0, d, dc, e).start()
+    for s in steps[1:]:
+        for axis in range(2):
+            table(axis, s).wait_recv()
+            spread(axis, s).wait_recv()
+            select(axis, s)
+        for axis, d, dc, e in pieces():
+            piece(axis, s, d, dc, e).start()
 
     def init(n, carry):
         cols = pl.ds(pl.multiple_of(n * wide, wide), wide)
@@ -391,10 +515,13 @@
     for j in range(n_grp):
         for e in range(local_exp):
             for r in order:
-                if local(j, r):
-                    dispatch(j, r, e).wait()
-                else:
-                    dispatch(j, r, e).wait_recv()
+                dy, dx, dc = plan[j][r]
+                for axis, (s, d) in enumerate(((dx, dy), (dy, dx))):
+                    cpy = piece(axis, s, d, dc, e)
+                    if d == 0 and dc == 0:
+                        cpy.wait()
+                    else:
+                        cpy.wait_recv()
 
             def up(n, carry, j=j, e=e):
                 cols = pl.ds(pl.multiple_of(n * 256, 256), 256)
@@ -416,7 +543,7 @@
                 giveback(j, r, e).start()
 
     for j in range(n_grp):
-        build(j, gmat, True)
+        build(j, gmat)
         for e in range(local_exp):
             for r in order:
                 if local(j, r):
@@ -451,8 +578,15 @@
         for r in range(per_grp):
             if not local(j, r):
                 for e in range(local_exp):
-                    dispatch(j, r, e).wait_send()
                     giveback(j, r, e).wait_send()
+    for axis in range(2):
+        for d in steps[1:]:
+            table(axis, d).wait_send()
+            spread(axis, d).wait_send()
+    for s in steps:
+        for axis, d, dc, e in pieces():
+            if d or dc:
+                piece(axis, s, d, dc, e).wait_send()
 
 
 def expert_layer(mesh, resid_h, expert_idx, gate_vals, w_gate, w_up, w_down):
@@ -466,7 +600,8 @@
     dims = (n_cp, n_x, top_k, experts, cap, local_exp)
     vm = pl.BlockSpec(memory_space=pltpu.VMEM)
     hb = pl.BlockSpec(memory_space=pl.ANY)
-    sems = [pltpu.SemaphoreType.DMA((n_cp, slots)) for _ in range(4)]
+    dma = pltpu.SemaphoreType.DMA
+    sems = [dma((2, n_x, slots)), dma((2, n_cp, slots)), dma((n_cp, slots)), dma((n_cp, slots))] + [dma((2, n_x - 1))] * 4
     return pl.pallas_call(
         functools.partial(moe_kernel, dims),
         out_shape=jax.ShapeDtypeStruct((rows, hidden), jnp.bfloat16),
@@ -476,11 +611,13 @@
             pltpu.VMEM((local_exp, hidden, ffn), jnp.bfloat16),
             pltpu.VMEM((local_exp, hidden, ffn), jnp.bfloat16),
             pltpu.VMEM((local_exp, ffn, hidden), jnp.bfloat16),
-            pltpu.VMEM((n_cp, slots, cap, hidden), jnp.bfloat16),
+            pltpu.VMEM((2, n_x, slots, cap, hidden // 2), jnp.bfloat16),
             pltpu.VMEM((n_cp, slots, cap, hidden), jnp.bfloat16),
             pltpu.VMEM((n_cp, slots, cap, hidden), jnp.bfloat16),
             pltpu.VMEM((experts, rows), jnp.float32),
             pltpu.VMEM((experts, rows), jnp.float32),
+            pltpu.VMEM((2, n_x - 1, experts, rows), jnp.float32),
+            pltpu.VMEM((2, n_x - 1, rows, hidden // 2), jnp.bfloat16),
             pltpu.VMEM((slots * cap, rows), jnp.float32),
             pltpu.VMEM((slots * cap, rows), jnp.float32),
             pltpu.VMEM((rows, hidden), jnp.float32),

time: 270 us -> 242 us (0.90)
  Pallas kernels: 253 us -> 240 us
  local copies, waits for them, and re-layouts: 14.5 us -> 2.09 us
    pallas_call x1, Pallas kernels: 166 us -> 145 us  [expert_layer(): pl.pallas_call(functools.partial(moe_kernel, dims), out_shape=jax.ShapeDt...]
    unnamed x6 -> x1, local copies, waits for them, and re-layouts: 11.7 us -> 2.09 us
    pallas_call x1, Pallas kernels: 86.9 us -> 94.7 us  [attention_residual(): pl.pallas_call(functools.partial(attn_kernel, (n_cp, n_x, hd)), out_shape...]
    reshape x1 -> x0, local copies, waits for them, and re-layouts: 2.82 us -> none  [attention_residual(): jnp.stack([w_query, w_key, w_value], axis=2).reshape(hidden, heads * 3 * hd)]
where the time goes in v3:
time: 242 us
  Pallas kernels  240 us (99%)
    pallas_call x1, Pallas kernels, expert_layer(): pl.pallas_call(functools.partial(moe_kernel, dims), out_shape=jax.ShapeDt...  145 us
    pallas_call x1, Pallas kernels, attention_residual(): pl.pallas_call(functools.partial(attn_kernel, (n_cp, n_x, hd)), out_shape...  94.7 us

profile of v3, /device:TPU:97, one launch (start us, length us, event | category | flops | bytes accessed | tf_op | source)
XLA Modules:
  0.0 241.7 jit_solution(11775482125290980816)
XLA Ops:
  0.0 94.7 %attn.1.h_in = bf16[192,2048]{1,0:T(8,128)(2,1)} custom-call(bf16[192,2048]{1,0:T(8,128)(2,1)} %x_in.1, bf16[4096,128]{1,0:T(8,128)(2,1)} %bitcast.6, bf16[4096,128]{1,0:T(8,128)(2,1)} %bitcast.7, bf16[4096,128]{1,0:T(8,128)(2,1)} %bitcast.8, bf16[256,2048]{1,0:T(8,128)(2,1)} %bitcast.9), custom_call_target="tpu_custom_call" | custom-call | tf_op jit(solution)/shard_map/attn/pallas_call | solution.py:335
  94.7 144.9 %moe.1 = bf16[192,2048]{1,0:T(8,128)(2,1)} custom-call(bf16[192,2048]{1,0:T(8,128)(2,1)} %attn.1.h_in, s32[8,192]{1,0:T(8,128)} %bitcast.10, f32[8,192]{1,0:T(8,128)} %bitcast.11, bf16[2,2048,1024]{2,1,0:T(8,128)(2,1)} %wg_hbm.1, bf16[2,2048,1024]{2,1,0:T(8,128)(2,1)} %wu_hbm.1, bf16[2,1024,2048]{2,1,0:T(8,128)(2,1)} %wd_hbm.1), custom_call_target="tpu_custom_call" | custom-call | tf_op jit(solution)/shard_map/moe/pallas_call | solution.py:605
  239.6 2.1 copy.12

commit v4 on v3

--- a/solution.py
+++ b/solution.py
@@ -80,34 +80,46 @@
     mask[0:blk, :] = jnp.where(k_pos + core * rows <= q_pos, 1.0, 0.0)
     mask[blk:, :] = jnp.where(k_pos + (1 - core) * rows <= q_pos, 1.0, 0.0)
 
-    def q_send(s, dy):
-        u = place(cp, nbr(-s))
-        return remote(snd.at[s, dy - 1], land.at[u], qs.at[s, dy - 1], qr.at[s, dy - 1], at_y((cp + dy) % n_cp))
-
-    def q_recv(s, dy):
-        u = place((cp - dy + n_cp) % n_cp, nbr(-s))
-        return remote(snd.at[s, dy - 1], land.at[u], qs.at[s, dy - 1], qr.at[s, dy - 1], at_y((cp + dy) % n_cp))
+    def span(p):
+        return pl.ds(0, rows) if p is None else parts[p]
+
+    def q_copy(s, p, dy, u):
+        at = span(p)
+        k = p or 0
+        return remote(snd.at[s, dy - 1, at], land.at[u, at], qs.at[s, k, dy - 1], qr.at[s, k, dy - 1], at_y((cp + dy) % n_cp))
+
+    def q_send(s, p, dy):
+        return q_copy(s, p, dy, place(cp, nbr(-s)))
+
+    def q_recv(s, p, dy):
+        return q_copy(s, p, dy, place((cp - dy + n_cp) % n_cp, nbr(-s)))
 
     def kv_send(s, dy):
         u = place((cp - dy + n_cp) % n_cp, nbr(-s))
         return remote(land.at[u, :, pl.ds(hd, 2 * hd)], kvp.at[u], ks.at[s, dy], kr.at[s, dy], partner)
 
-    def project(s):
+    def project(s, p=None):
+        at = span(p)
         for dy in (1, n_cp - 1, 2, 0):
             i = (cp + dy) % n_cp
             cols = pl.ds(pl.multiple_of((i % 2) * 3 * hd, 3 * hd), 3 * hd)
-            xv = x_in[...] if s == 0 else xbuf[s - 1]
+            xv = x_in[at] if s == 0 else xbuf[s - 1, at]
             res = jnp.dot(xv, wall[i // 2, :, cols], preferred_element_type=f32).astype(bf)
             if dy:
-                snd[s, dy - 1] = res
-                q_send(s, dy).start()
+                snd[s, dy - 1, at] = res
+                q_send(s, p, dy).start()
             else:
-                land[place(cp, nbr(-s))] = res
-                kv_send(s, 0).start()
+                land[place(cp, nbr(-s)), at] = res
+                if p is None or (s, p) in ((1, 1), (n_x - 1, 0)):
+                    kv_send(s, 0).start()
+
+    def halves(s):
+        return (0, 1) if s in (1, n_x - 1) else (None,)
 
     def relay(s):
         for dy in (1, n_cp - 1, 2):
-            q_recv(s, dy).wait_recv()
+            for p in halves(s):
+                q_recv(s, p, dy).wait_recv()
             kv_send(s, dy).start()
 
     x_own(1, 0).wait_recv()
@@ -117,9 +129,9 @@
     w_part.wait_recv()
     project(0)
 
-    w_mid = wo.shape[0] // 2
-    w_qtr = w_mid // n_cp
-    w_cut = w_mid * 5 // 8
+    w_mid = wo.shape[0] * 3 // 4
+    w_qtr = (wo.shape[0] - w_mid) // n_cp
+    w_cut = w_mid // 2
     tp_at = lambda s: nbr(-s) * 2 + core
 
     def w_rows(p, y):
@@ -143,21 +155,24 @@
         return remote(blk_ref, blk_ref, ys.at[s - 1, dy - 1], yr.at[s - 1, dy - 1], at_y((cp + dy) % n_cp))
 
     def w_pass(s, p):
-        blk_ref = wfull.at[tp_at(s), pl.ds(p * w_mid, w_mid)]
+        blk_ref = wfull.at[tp_at(s), pl.ds(p * w_mid, w_mid if p == 0 else wo.shape[0] - w_mid)]
         return remote(blk_ref, blk_ref, ps.at[s, p], pr.at[s, p], partner)
 
     relays = ((1, 0), (-1, 1), (-1, 2))
-    own_sends = ((1, 0), (-1, 1), (-1, 2), (1, 1), (-1, 0), (1, 2))
+    own_sends = ((1, 0), (-1, 2), (-1, 1), (1, 2), (-1, 0), (1, 1))
     y_offs = (1, n_cp - 1, 2)
 
-    def w_step1():
+    def w_step0():
         for d, p in relays:
             w_own(d, p).wait_recv()
             w_fwd(d, p).start()
+        for dy in y_offs:
+            w_share(n_x - 1, dy).start()
+
+    def w_step1():
         w_own(1, 2).wait_recv()
         for dy in y_offs:
             w_share(1, dy).start()
-            w_share(n_x - 1, dy).start()
         w_own(1, 1).wait_recv()
         w_own(-1, 0).wait_recv()
         w_pass(1, 0).start()
@@ -187,10 +202,12 @@
     for p in range(2):
         w_pass(0, p).start()
 
+    project(1, 0)
+    project(n_x - 1, 1)
     x_own(1, 1).wait_recv()
-    project(1)
+    project(1, 1)
     x_own(-1, 0).wait_recv()
-    project(n_x - 1)
+    project(n_x - 1, 0)
     relay(0)
     x_fwd(1).wait_recv()
     x_fwd(-1).wait_recv()
@@ -200,6 +217,7 @@
     for s in range(n_x):
         for dy in range(n_cp):
             kv_send(s, dy).wait_recv()
+    w_step0()
 
     c_exp = hd ** -0.5 * 1.4426950408889634
     nt = (((1,), (1,)), ((), ()))
@@ -234,13 +252,14 @@
         if masked:
             s1 = jnp.where(mask[0:blk, :] > 0.5, s1, -1e30)
             s2 = jnp.where(mask[blk:, :] > 0.5, s2, -1e30)
-        top = jnp.maximum(jnp.max(s1, axis=0, keepdims=True), jnp.max(s2, axis=0, keepdims=True))
-        new = jnp.maximum(mx, top)
+        m1 = jnp.maximum(mx, jnp.max(s1, axis=0, keepdims=True))
+        p1 = jnp.exp2((s1 - m1) * c_exp)
+        new = jnp.maximum(m1, jnp.max(s2, axis=0, keepdims=True))
+        p2 = jnp.exp2((s2 - new) * c_exp)
         keep = jnp.exp2((mx - new) * c_exp)
-        p1 = jnp.exp2((s1 - new) * c_exp)
-        p2 = jnp.exp2((s2 - new) * c_exp)
-        den = den * keep + jnp.sum(p1, axis=0, keepdims=True) + jnp.sum(p2, axis=0, keepdims=True)
-        acc = acc * keep + jnp.dot(vt[0, :, cols], p1.astype(bf), preferred_element_type=f32) + jnp.dot(vt[1, :, cols], p2.astype(bf), preferred_element_type=f32)
+        mend = jnp.exp2((m1 - new) * c_exp)
+        den = den * keep + jnp.sum(p1, axis=0, keepdims=True) * mend + jnp.sum(p2, axis=0, keepdims=True)
+        acc = acc * keep + jnp.dot(vt[0, :, cols], p1.astype(bf), preferred_element_type=f32) * mend + jnp.dot(vt[1, :, cols], p2.astype(bf), preferred_element_type=f32)
         return new, den, acc
 
     def attend(b, carry):
@@ -249,7 +268,8 @@
 
         start = (jnp.full((1, blk), -1e30, f32), jnp.zeros((1, blk), f32), jnp.zeros((hd, blk), f32))
         start = step(b, b, start, True)
-        mx, den, acc = lax.fori_loop(0, b, lambda t, c: step(b, t, c, False), start)
+        start = lax.fori_loop(0, b // 2, lambda t, c: step(b, 2 * t + 1, step(b, 2 * t, c, False), False), start)
+        mx, den, acc = lax.fori_loop(b // 2 * 2, b, lambda t, c: step(b, t, c, False), start)
         o = (acc / den).T.astype(bf)
         for u in range(units):
             cpy, own, cols = o_copy(b, u)
@@ -302,7 +322,8 @@
         for dy in range(n_cp):
             kv_send(s, dy).wait_send()
             if dy:
-                q_send(s, dy).wait_send()
+                for p in halves(s):
+                    q_send(s, p, dy).wait_send()
 
     def drain(b, carry):
         for u in range(units):
@@ -316,7 +337,7 @@
     lax.fori_loop(0, 2 * n_cp, drain, 0)
 
 
-RELAY_AT = (3, 5, 7)
+RELAY_AT = (4, 6, 7)
 
 
 def attention_residual(mesh, hidden_in, w_query, w_key, w_value, w_out):
@@ -351,7 +372,7 @@
             pltpu.VMEM((rows, n_units * hd), bf),
             pltpu.VMEM((2 * n_x, heads * hd, hidden), bf),
             dma((4,)), dma((n_x - 1, 2)), dma((n_x - 1, 2)), dma((n_x - 1, 3)), dma((n_x - 1, 3)),
-            dma((n_x, n_cp - 1)), dma((n_x, n_cp - 1)), dma((n_x, n_cp)), dma((n_x, n_cp)),
+            dma((n_x, 2, n_cp - 1)), dma((n_x, 2, n_cp - 1)), dma((n_x, n_cp)), dma((n_x, n_cp)),
             dma((n_units,)), dma((n_units,)), dma((1,)), dma((1,)), dma((n_x, 2)), dma((n_x, 2)),
             dma((n_x - 1, n_cp - 1)), dma((n_x - 1, n_cp - 1)),
         ],

time: 242 us -> 231 us (0.955)
  Pallas kernels: 240 us -> 229 us
    pallas_call x1, Pallas kernels: 94.7 us -> 84.4 us  [attention_residual(): pl.pallas_call(functools.partial(attn_kernel, (n_cp, n_x, hd)), out_shape...]
where the time goes in v4:
time: 231 us
  Pallas kernels  229 us (99%)
    pallas_call x1, Pallas kernels, expert_layer(): pl.pallas_call(functools.partial(moe_kernel, dims), out_shape=jax.ShapeDt...  145 us
    pallas_call x1, Pallas kernels, attention_residual(): pl.pallas_call(functools.partial(attn_kernel, (n_cp, n_x, hd)), out_shape...  84.4 us

profile of v4, /device:TPU:97, one launch (start us, length us, event | category | flops | bytes accessed | tf_op | source)
XLA Modules:
  0.0 231.1 jit_solution(7910473741459148275)
XLA Ops:
  0.0 84.4 %attn.1.h_in = bf16[192,2048]{1,0:T(8,128)(2,1)} custom-call(bf16[192,2048]{1,0:T(8,128)(2,1)} %x_in.1, bf16[4096,128]{1,0:T(8,128)(2,1)} %bitcast.6, bf16[4096,128]{1,0:T(8,128)(2,1)} %bitcast.7, bf16[4096,128]{1,0:T(8,128)(2,1)} %bitcast.8, bf16[256,2048]{1,0:T(8,128)(2,1)} %bitcast.9), custom_call_target="tpu_custom_call" | custom-call | tf_op jit(solution)/shard_map/attn/pallas_call | solution.py:356
  84.4 144.6 %moe.1 = bf16[192,2048]{1,0:T(8,128)(2,1)} custom-call(bf16[192,2048]{1,0:T(8,128)(2,1)} %attn.1.h_in, s32[8,192]{1,0:T(8,128)} %bitcast.10, f32[8,192]{1,0:T(8,128)} %bitcast.11, bf16[2,2048,1024]{2,1,0:T(8,128)(2,1)} %wg_hbm.1, bf16[2,2048,1024]{2,1,0:T(8,128)(2,1)} %wu_hbm.1, bf16[2,1024,2048]{2,1,0:T(8,128)(2,1)} %wd_hbm.1), custom_call_target="tpu_custom_call" | custom-call | tf_op jit(solution)/shard_map/moe/pallas_call | solution.py:626
  229.0 2.1 copy.12

commit v5 on v4

--- a/solution.py
+++ b/solution.py
@@ -231,14 +231,12 @@
         own = jnp.logical_and(dst_cp == cp, dst_x == x_pos)
         return cpy, own, cols
 
-    def flip(b, carry):
+    def flip(b):
         own_u = pl.ds(b * units, units)
         cols = pl.ds(pl.multiple_of(b * blk, blk), blk)
         vt[0, :, cols] = land[own_u, :, 2 * hd:3 * hd].reshape(blk, hd).T
         vt[1, :, cols] = kvp[own_u, :, hd:2 * hd].reshape(blk, hd).T
-        return carry
-
-    lax.fori_loop(0, 2 * n_cp, flip, 0)
+
 
     def step(b, t, carry, masked):
         mx, den, acc = carry
@@ -267,6 +265,7 @@
             pl.when(b == at)(todo)
 
         start = (jnp.full((1, blk), -1e30, f32), jnp.zeros((1, blk), f32), jnp.zeros((hd, blk), f32))
+        flip(b)
         start = step(b, b, start, True)
         start = lax.fori_loop(0, b // 2, lambda t, c: step(b, 2 * t + 1, step(b, 2 * t, c, False), False), start)
         mx, den, acc = lax.fori_loop(b // 2 * 2, b, lambda t, c: step(b, t, c, False), start)
@@ -382,7 +381,7 @@
 
 
 def moe_kernel(dims, h_in, idx_ref, gate_ref, wg_hbm, wu_hbm, wd_hbm, y_ref,
-               wg, wu, wd, send, recv, ret, slots, gates, tabs, held, dmat, gmat, acc, hid,
+               wg, wu, wd, send, recv, ret, slots, gates, tabs, held, dmat, gmat, gsp, acc, hid,
                wsem, ssem, rsem, bsem, csem, tsem, tgot, hsem, hgot):
     n_cp, n_x, top_k, experts, cap, local_exp = dims
     per_grp = 2 * n_x
@@ -456,9 +455,20 @@
         c, t = peer(axis, d, 0)
         return pltpu.make_async_remote_copy(slots, tabs.at[axis, d - 1], tsem.at[axis, d - 1], tgot.at[axis, d - 1], device_id={'cp': c, 'tp': t}, device_id_type=MESH)
 
-    def spread(axis, d):
+    h_half = rows // 2
+    h_parts = (pl.ds(0, h_half), pl.ds(h_half, h_half))
+
+    def spread(axis, d, p):
         c, t = peer(axis, d, 0)
-        return pltpu.make_async_remote_copy(h_in.at[:, cols_of[axis]], held.at[axis, d - 1], hsem.at[axis, d - 1], hgot.at[axis, d - 1], device_id={'cp': c, 'tp': t}, device_id_type=MESH)
+        return pltpu.make_async_remote_copy(h_in.at[h_parts[p], cols_of[axis]], held.at[axis, d - 1, h_parts[p]], hsem.at[axis, d - 1, p], hgot.at[axis, d - 1, p], device_id={'cp': c, 'tp': t}, device_id_type=MESH)
+
+    def onward(axis, p):
+        d = (1, n_x - 1)[p]
+        c, t = peer(axis, d, 0)
+        return pltpu.make_async_remote_copy(held.at[axis, d - 1, h_parts[p]], held.at[axis, 1, h_parts[p]], hsem.at[axis, 1, p], hgot.at[axis, 1, p], device_id={'cp': c, 'tp': t}, device_id_type=MESH)
+
+    spreads = [(axis, d, p) for d, p in ((1, 0), (n_x - 1, 1), (1, 1), (n_x - 1, 0)) for axis in range(2)]
+    onwards = [(axis, p) for p in range(2) for axis in range(2)]
 
     def piece(axis, s, d, dc, e):
         c, t = peer(1 - axis, d, dc)
@@ -505,21 +515,27 @@
     half = per_grp * cap
     wide = 512
     order = range(per_grp)
-    for axis in range(2):
-        select(axis, 0)
     pl.semaphore_wait(barrier, n_grp * per_grp - 1)
+    for axis, d, p in spreads:
+        spread(axis, d, p).start()
     for d in steps[1:]:
         for axis in range(2):
             table(axis, d).start()
-    for d in steps[1:]:
-        for axis in range(2):
-            spread(axis, d).start()
+    for axis in range(2):
+        select(axis, 0)
+    for axis, p in onwards:
+        spread(axis, (1, n_x - 1)[p], p).wait_recv()
+        onward(axis, p).start()
     for axis, d, dc, e in pieces():
         piece(axis, 0, d, dc, e).start()
     for s in steps[1:]:
         for axis in range(2):
             table(axis, s).wait_recv()
-            spread(axis, s).wait_recv()
+            if s == 2:
+                for p in range(2):
+                    onward(axis, p).wait_recv()
+            else:
+                spread(axis, s, 1 if s == 1 else 0).wait_recv()
             select(axis, s)
         for axis, d, dc, e in pieces():
             piece(axis, s, d, dc, e).start()
@@ -565,6 +581,13 @@
 
     for j in range(n_grp):
         build(j, gmat)
+        g0 = gmat[...].T
+        hi = g0.astype(jnp.bfloat16)
+        g1 = g0 - hi.astype(jnp.float32)
+        mid_g = g1.astype(jnp.bfloat16)
+        gsp[0] = hi
+        gsp[1] = mid_g
+        gsp[2] = (g1 - mid_g.astype(jnp.float32)).astype(jnp.bfloat16)
         for e in range(local_exp):
             for r in order:
                 if local(j, r):
@@ -574,16 +597,10 @@
 
         def comb(n, carry, j=j):
             cols = pl.ds(pl.multiple_of(n * wide, wide), wide)
-            g0 = gmat[...]
-            hi = g0.astype(jnp.bfloat16)
-            g1 = g0 - hi.astype(jnp.float32)
-            mid = g1.astype(jnp.bfloat16)
-            lo = (g1 - mid.astype(jnp.float32)).astype(jnp.bfloat16)
             z = ret[j, :, :, cols].reshape(grp_rows, wide)
-            dims_t = (((0,), (0,)), ((), ()))
-            tot = lax.dot_general(lo, z, dims_t, preferred_element_type=jnp.float32)
-            tot = tot + lax.dot_general(mid, z, dims_t, preferred_element_type=jnp.float32)
-            tot = tot + lax.dot_general(hi, z, dims_t, preferred_element_type=jnp.float32)
+            tot = jnp.dot(gsp[2], z, preferred_element_type=jnp.float32)
+            tot = tot + jnp.dot(gsp[1], z, preferred_element_type=jnp.float32)
+            tot = tot + jnp.dot(gsp[0], z, preferred_element_type=jnp.float32)
             acc[:, cols] += tot
             return carry
 
@@ -603,7 +620,10 @@
     for axis in range(2):
         for d in steps[1:]:
             table(axis, d).wait_send()
-            spread(axis, d).wait_send()
+        for p in range(2):
+            onward(axis, p).wait_send()
+    for axis, d, p in spreads:
+        spread(axis, d, p).wait_send()
     for s in steps:
         for axis, d, dc, e in pieces():
             if d or dc:
@@ -622,7 +642,7 @@
     vm = pl.BlockSpec(memory_space=pltpu.VMEM)
     hb = pl.BlockSpec(memory_space=pl.ANY)
     dma = pltpu.SemaphoreType.DMA
-    sems = [dma((2, n_x, slots)), dma((2, n_cp, slots)), dma((n_cp, slots)), dma((n_cp, slots))] + [dma((2, n_x - 1))] * 4
+    sems = [dma((2, n_x, slots)), dma((2, n_cp, slots)), dma((n_cp, slots)), dma((n_cp, slots))] + [dma((2, n_x - 1))] * 2 + [dma((2, n_x - 1, 2))] * 2
     return pl.pallas_call(
         functools.partial(moe_kernel, dims),
         out_shape=jax.ShapeDtypeStruct((rows, hidden), jnp.bfloat16),
@@ -641,6 +661,7 @@
             pltpu.VMEM((2, n_x - 1, rows, hidden // 2), jnp.bfloat16),
             pltpu.VMEM((slots * cap, rows), jnp.float32),
             pltpu.VMEM((slots * cap, rows), jnp.float32),
+            pltpu.VMEM((3, rows, slots * cap), jnp.bfloat16),
             pltpu.VMEM((rows, hidden), jnp.float32),
             pltpu.VMEM((2 * n_x * cap, ffn), jnp.bfloat16),
             pltpu.SemaphoreType.DMA((3,)),

time: 231 us -> 227 us (0.983)
  Pallas kernels: 229 us -> 225 us
    pallas_call x1, Pallas kernels: 145 us -> 140 us  [expert_layer(): pl.pallas_call(functools.partial(moe_kernel, dims), out_shape=jax.ShapeDt...]
where the time goes in v5:
time: 227 us
  Pallas kernels  225 us (99%)
    pallas_call x1, Pallas kernels, expert_layer(): pl.pallas_call(functools.partial(moe_kernel, dims), out_shape=jax.ShapeDt...  140 us
    pallas_call x1, Pallas kernels, attention_residual(): pl.pallas_call(functools.partial(attn_kernel, (n_cp, n_x, hd)), out_shape...  84.8 us

profile of v5, /device:TPU:97, one launch (start us, length us, event | category | flops | bytes accessed | tf_op | source)
XLA Modules:
  0.0 226.9 jit_solution(4518092962974805143)
XLA Ops:
  0.0 84.8 %attn.1.h_in = bf16[192,2048]{1,0:T(8,128)(2,1)} custom-call(bf16[192,2048]{1,0:T(8,128)(2,1)} %x_in.1, bf16[4096,128]{1,0:T(8,128)(2,1)} %bitcast.6, bf16[4096,128]{1,0:T(8,128)(2,1)} %bitcast.7, bf16[4096,128]{1,0:T(8,128)(2,1)} %bitcast.8, bf16[256,2048]{1,0:T(8,128)(2,1)} %bitcast.9), custom_call_target="tpu_custom_call" | custom-call | tf_op jit(solution)/shard_map/attn/pallas_call | solution.py:355
  84.8 140.0 %moe.1 = bf16[192,2048]{1,0:T(8,128)(2,1)} custom-call(bf16[192,2048]{1,0:T(8,128)(2,1)} %attn.1.h_in, s32[8,192]{1,0:T(8,128)} %bitcast.10, f32[8,192]{1,0:T(8,128)} %bitcast.11, bf16[2,2048,1024]{2,1,0:T(8,128)(2,1)} %wg_hbm.1, bf16[2,2048,1024]{2,1,0:T(8,128)(2,1)} %wu_hbm.1, bf16[2,1024,2048]{2,1,0:T(8,128)(2,1)} %wd_hbm.1), custom_call_target="tpu_custom_call" | custom-call | tf_op jit(solution)/shard_map/moe/pallas_call | solution.py:646
  224.8 2.1 copy.12

commit v6 on v5

--- a/solution.py
+++ b/solution.py
@@ -381,7 +381,7 @@
 
 
 def moe_kernel(dims, h_in, idx_ref, gate_ref, wg_hbm, wu_hbm, wd_hbm, y_ref,
-               wg, wu, wd, send, recv, ret, slots, gates, tabs, held, dmat, gmat, gsp, acc, hid,
+               wg, wu, wd, send, recv, ret, slots, gates, slots16, slots_of, tabs, held, dmat, gmat, gsp, acc, hid,
                wsem, ssem, rsem, bsem, csem, tsem, tgot, hsem, hgot):
     n_cp, n_x, top_k, experts, cap, local_exp = dims
     per_grp = 2 * n_x
@@ -429,6 +429,7 @@
     before = jnp.where(lax.broadcasted_iota(jnp.int32, (rows, rows), 0) < lax.broadcasted_iota(jnp.int32, (rows, rows), 1), 1.0, 0.0)
     count = jnp.dot(hit.astype(jnp.bfloat16), before.astype(jnp.bfloat16), preferred_element_type=jnp.float32)
     slots[...] = jnp.where(hit > 0.5, count, -1.0)
+    slots16[...] = slots[...].astype(jnp.bfloat16)
     gates[...] = gsel
     c_iota = lax.broadcasted_iota(jnp.int32, (cap, rows), 0).astype(jnp.float32)
 
@@ -453,7 +454,7 @@
 
     def table(axis, d):
         c, t = peer(axis, d, 0)
-        return pltpu.make_async_remote_copy(slots, tabs.at[axis, d - 1], tsem.at[axis, d - 1], tgot.at[axis, d - 1], device_id={'cp': c, 'tp': t}, device_id_type=MESH)
+        return pltpu.make_async_remote_copy(slots16, tabs.at[axis, d - 1], tsem.at[axis, d - 1], tgot.at[axis, d - 1], device_id={'cp': c, 'tp': t}, device_id_type=MESH)
 
     h_half = rows // 2
     h_parts = (pl.ds(0, h_half), pl.ds(h_half, h_half))
@@ -484,7 +485,9 @@
         return [(axis, d, dc, e) for e in range(local_exp) for dc in range(2) for d in steps for axis in range(2)]
 
     def select(axis, s):
-        tab = slots if s == 0 else tabs.at[axis, s - 1]
+        tab = slots if s == 0 else slots_of
+        if s:
+            slots_of[...] = tabs[axis, s - 1].astype(jnp.float32)
         for d in range(n_x):
             for dc in range(2):
                 c, t = peer(1 - axis, d, dc)
@@ -601,17 +604,14 @@
             tot = jnp.dot(gsp[2], z, preferred_element_type=jnp.float32)
             tot = tot + jnp.dot(gsp[1], z, preferred_element_type=jnp.float32)
             tot = tot + jnp.dot(gsp[0], z, preferred_element_type=jnp.float32)
-            acc[:, cols] += tot
+            if j == n_grp - 1:
+                y_ref[:, cols] = (acc[:, cols] + tot).astype(jnp.bfloat16)
+            else:
+                acc[:, cols] += tot
             return carry
 
         lax.fori_loop(0, hidden // wide, comb, 0)
 
-    def fin(n, carry):
-        cols = pl.ds(pl.multiple_of(n * wide, wide), wide)
-        y_ref[:, cols] = acc[:, cols].astype(jnp.bfloat16)
-        return carry
-
-    lax.fori_loop(0, hidden // wide, fin, 0)
     for j in range(n_grp):
         for r in range(per_grp):
             if not local(j, r):
@@ -657,7 +657,9 @@
             pltpu.VMEM((n_cp, slots, cap, hidden), jnp.bfloat16),
             pltpu.VMEM((experts, rows), jnp.float32),
             pltpu.VMEM((experts, rows), jnp.float32),
-            pltpu.VMEM((2, n_x - 1, experts, rows), jnp.float32),
+            pltpu.VMEM((experts, rows), jnp.bfloat16),
+            pltpu.VMEM((experts, rows), jnp.float32),
+            pltpu.VMEM((2, n_x - 1, experts, rows), jnp.bfloat16),
             pltpu.VMEM((2, n_x - 1, rows, hidden // 2), jnp.bfloat16),
             pltpu.VMEM((slots * cap, rows), jnp.float32),
             pltpu.VMEM((slots * cap, rows), jnp.float32),

time: 227 us -> 226 us (level)
  no operation moved by 1% of the time
where the time goes in v6:
time: 226 us
  Pallas kernels  223 us (99%)
    pallas_call x1, Pallas kernels, expert_layer(): pl.pallas_call(functools.partial(moe_kernel, dims), out_shape=jax.ShapeDt...  139 us
    pallas_call x1, Pallas kernels, attention_residual(): pl.pallas_call(functools.partial(attn_kernel, (n_cp, n_x, hd)), out_shape...  84.8 us

profile of v6, /device:TPU:97, one launch (start us, length us, event | category | flops | bytes accessed | tf_op | source)
XLA Modules:
  0.0 225.6 jit_solution(17917954233145534635)
XLA Ops:
  0.0 84.8 %attn.1.h_in = bf16[192,2048]{1,0:T(8,128)(2,1)} custom-call(bf16[192,2048]{1,0:T(8,128)(2,1)} %x_in.1, bf16[4096,128]{1,0:T(8,128)(2,1)} %bitcast.6, bf16[4096,128]{1,0:T(8,128)(2,1)} %bitcast.7, bf16[4096,128]{1,0:T(8,128)(2,1)} %bitcast.8, bf16[256,2048]{1,0:T(8,128)(2,1)} %bitcast.9), custom_call_target="tpu_custom_call" | custom-call | tf_op jit(solution)/shard_map/attn/pallas_call | solution.py:355
  84.8 138.7 %moe.1 = bf16[192,2048]{1,0:T(8,128)(2,1)} custom-call(bf16[192,2048]{1,0:T(8,128)(2,1)} %attn.1.h_in, s32[8,192]{1,0:T(8,128)} %bitcast.10, f32[8,192]{1,0:T(8,128)} %bitcast.11, bf16[2,2048,1024]{2,1,0:T(8,128)(2,1)} %wg_hbm.1, bf16[2,2048,1024]{2,1,0:T(8,128)(2,1)} %wu_hbm.1, bf16[2,1024,2048]{2,1,0:T(8,128)(2,1)} %wd_hbm.1), custom_call_target="tpu_custom_call" | custom-call | tf_op jit(solution)/shard_map/moe/pallas_call | solution.py:646
  223.5 2.1 copy.12

commit v7 on v6

--- a/solution.py
+++ b/solution.py
@@ -482,7 +482,7 @@
         return pltpu.make_async_remote_copy(src, dst, ssem.at[axis, s, k], got, device_id={'cp': c, 'tp': t}, device_id_type=MESH)
 
     def pieces():
-        return [(axis, d, dc, e) for e in range(local_exp) for dc in range(2) for d in steps for axis in range(2)]
+        return [(axis, d, dc, e) for e in range(local_exp) for d in (2, 1, n_x - 1, 0) for dc in range(2) for axis in range(2)]
 
     def select(axis, s):
         tab = slots if s == 0 else slots_of

time: 226 us -> 226 us (level)
  no operation moved by 1% of the time
where the time goes in v7:
time: 226 us
  Pallas kernels  224 us (99%)
    pallas_call x1, Pallas kernels, expert_layer(): pl.pallas_call(functools.partial(moe_kernel, dims), out_shape=jax.ShapeDt...  139 us
    pallas_call x1, Pallas kernels, attention_residual(): pl.pallas_call(functools.partial(attn_kernel, (n_cp, n_x, hd)), out_shape...  84.8 us

profile of v7, /device:TPU:97, one launch (start us, length us, event | category | flops | bytes accessed | tf_op | source)
XLA Modules:
  0.0 225.6 jit_solution(16680266839569063452)
XLA Ops:
  0.0 84.8 %attn.1.h_in = bf16[192,2048]{1,0:T(8,128)(2,1)} custom-call(bf16[192,2048]{1,0:T(8,128)(2,1)} %x_in.1, bf16[4096,128]{1,0:T(8,128)(2,1)} %bitcast.6, bf16[4096,128]{1,0:T(8,128)(2,1)} %bitcast.7, bf16[4096,128]{1,0:T(8,128)(2,1)} %bitcast.8, bf16[256,2048]{1,0:T(8,128)(2,1)} %bitcast.9), custom_call_target="tpu_custom_call" | custom-call | tf_op jit(solution)/shard_map/attn/pallas_call | solution.py:355
  84.8 138.8 %moe.1 = bf16[192,2048]{1,0:T(8,128)(2,1)} custom-call(bf16[192,2048]{1,0:T(8,128)(2,1)} %attn.1.h_in, s32[8,192]{1,0:T(8,128)} %bitcast.10, f32[8,192]{1,0:T(8,128)} %bitcast.11, bf16[2,2048,1024]{2,1,0:T(8,128)(2,1)} %wg_hbm.1, bf16[2,2048,1024]{2,1,0:T(8,128)(2,1)} %wu_hbm.1, bf16[2,1024,2048]{2,1,0:T(8,128)(2,1)} %wd_hbm.1), custom_call_target="tpu_custom_call" | custom-call | tf_op jit(solution)/shard_map/moe/pallas_call | solution.py:646
  223.5 2.1 copy.12
